TPU v7x, 512 devices: a whole 4x8x8 slice. The times are simulated.
512 devices in a mesh: prow: 16 (over z, core), pcol: 32 (over y, x).
Axes of the slice: x: 4, y: 8, z: 8, core: 2. Of those that a mesh axis runs over, the one named last changes fastest.
Arguments:
- tiles: bfloat16 [16, 32, 32, 256, 256], P('prow', 'pcol')
- tile_brow: int32 [16, 32, 32], P('prow', 'pcol'), may hold values from 0 to 31, as said below
- tile_bcol: int32 [16, 32, 32], P('prow', 'pcol'), may hold values from 0 to 15, as said below
- tile_count: int32 [16, 32], P('prow', 'pcol'), may hold values from 8 to 32, as said below
Outputs:
- row_scale: float32 [32, 16, 256], P(None, 'prow')
- col_scale: float32 [16, 32, 256], P(None, 'pcol')
Inputs may be any that keep to these rules, and one draw needn't show every extreme that they name: `tile_brow`: on one device, no two slots name the same pair of local block row and column; the diagonal tile of every block row is present and live, in the first slots of the device that holds it. `tile_bcol`: see tile_brow. `tile_count`: a device that holds diagonal tiles has all 32 slots live, every other device at most 16.
All inputs are finite; a program needn't handle non-finite values.
Results may differ from a plain program's by a relative error of at most 0.0003.
Values sent between devices are 32-bit elements; how exact they have to be, the bound alone decides.
No kernel may reach another device: no remote copies, remote signals or barrier semaphores. Data moves between devices by JAX's collectives and lax.ppermute only.
A program may use at most 64 MiB of HBM per device.

v0:
```python
import jax
import jax.numpy as jnp
from jax import lax
from jax.sharding import Mesh
from jax.sharding import PartitionSpec as P

BR_DEV = 32
SWEEPS = 3
PCOL = ("pcol_0", "pcol_1")


def one_axis_at_a_time(value, axes):
    for axis in axes:
        value = lax.pmax(value, axis)
    return value


def from_everyone(value, axis):
    devices = lax.axis_size(axis)
    return lax.all_to_all(
        jnp.broadcast_to(value[None], (devices, *value.shape)), axis, 0, 0, tiled=True
    )


def taken_together(value, axis):
    everything = from_everyone(value, axis)
    return jnp.max(everything, axis=0)


def rescale(scale, largest):
    return scale / jnp.sqrt(largest)


def on_device(tiles, tile_brow, tile_bcol, tile_count):
    slots = tiles.shape[2]
    width = tiles.shape[3]
    col_blocks = BR_DEV * lax.axis_size("prow") // lax.axis_size(PCOL)
    brow = tile_brow.reshape(slots)
    bcol = tile_bcol.reshape(slots)
    alive = (jnp.arange(slots, dtype=jnp.int32) < tile_count.reshape(1)).astype(jnp.float32)
    block = tiles.reshape(slots, width, width)
    row_vec = jnp.ones((BR_DEV, width), jnp.float32)
    col_vec = jnp.ones((col_blocks, width), jnp.float32)
    for sweep in range(SWEEPS):
        scaled = (
            jnp.abs(block.astype(jnp.float32))
            * row_vec[brow][:, :, None]
            * col_vec[bcol][:, None, :]
        )
        row_part = jnp.max(scaled, axis=2) * alive[:, None]
        col_part = jnp.max(scaled, axis=1) * alive[:, None]
        row_local = jnp.zeros((BR_DEV, width), jnp.float32).at[brow].max(row_part)
        col_local = jnp.zeros((col_blocks, width), jnp.float32).at[bcol].max(col_part)
        row_max = one_axis_at_a_time(row_local, PCOL)
        col_max = taken_together(col_local, "prow")
        row_vec = rescale(row_vec, row_max)
        col_vec = rescale(col_vec, col_max)
    return (row_vec.reshape(BR_DEV, 1, width), col_vec.reshape(col_blocks, 1, width))


def solution(mesh):
    finer = Mesh(mesh.devices.reshape(mesh.shape["prow"], 8, 4), ("prow", "pcol_0", "pcol_1"))
    in_specs = (
        P("prow", PCOL, None, None, None),
        P("prow", PCOL, None),
        P("prow", PCOL, None),
        P("prow", PCOL),
    )
    out_specs = (P(None, "prow", None), P(None, PCOL, None))
    return jax.shard_map(
        on_device, mesh=finer, in_specs=in_specs, out_specs=out_specs, check_vma=False
    )
```

profile of v0, /device:TPU:64, one launch (start us, length us, event | category | flops | bytes accessed | tf_op | source)
XLA Modules:
  0.0 187.4 jit_solution(17565205156358958719)
XLA Ops:
  0.6 0.7 fusion.33
  1.3 0.7 fusion.34
  2.6 0.6 gather_fusion.1
  3.3 0.6 gather_fusion
  3.9 5.1 %fusion.8 = (f32[32,256]{1,0:T(8,128)S(1)}, f32[32,256]{1,0:T(8,128)S(1)}) fusion(bf16[1,1,32,256,256]{4,3,2,1,0:T(8,128)(2,1)} %param.4, f32[32,256]{1,0:T(8,128)S(1)} %gather_fusion.1, f32[32,256]{1,0:T(8,128)S(1)} %gather_fusion), kind=kLoop, calls=%fused_computation.24 | loop fusion | flops 12566528 | bytes 4325376 | tf_op jit(solution)/shard_map/reduce_max | solution.py:50
  9.0 0.8 scatter_custom_fusion.1
  9.8 0.7 broadcast_in_dim.12
  10.5 10.0 %all-to-all-start = ((f32[16,16,256]{2,1,0:T(8,128)}), f32[16,16,256]{2,1,0:T(8,128)S(1)}, u32[]{:S(2)}, u32[]{:S(2)}) async-start(f32[16,16,256]{2,1,0:T(8,128)} %broadcast_in_dim.12), calls=%async_computation | async-start | bytes 524288 | tf_op jit(solution)/shard_map/all_to_all | solution.py:20
  20.5 0.8 scatter_custom_fusion
  21.3 30.4 %pmax.42 = f32[32,256]{1,0:T(8,128)S(1)} all-reduce(f32[32,256]{1,0:T(8,128)S(1)} %scatter_custom_fusion), channel_id=1, replica_groups=mesh['prow'=16,'pcol_0'=8,'pcol_1'=4] {'pcol_0'}, use_global_device_ids=true, to_apply=%region_2.0 | all-reduce | flops 8192 | bytes 65536 | tf_op jit(solution)/shard_map/pmax | solution.py:14
  51.7 17.1 %pmax.43 = f32[32,256]{1,0:T(8,128)S(1)} all-reduce(f32[32,256]{1,0:T(8,128)S(1)} %pmax.42), channel_id=1, replica_groups=mesh['prow'=16,'pcol_0'=8,'pcol_1'=4] {'pcol_1'}, use_global_device_ids=true, to_apply=%region_3.0 | all-reduce | flops 8192 | bytes 65536 | tf_op jit(solution)/shard_map/pmax | solution.py:14
  68.8 0.6 gather_fusion.2
  69.4 0.0 all-to-all-done
  69.4 0.6 gather_fusion.3
  70.0 5.1 %fusion.5 = (f32[32,256]{1,0:T(8,128)S(1)}, f32[32,256]{1,0:T(8,128)S(1)}) fusion(bf16[1,1,32,256,256]{4,3,2,1,0:T(8,128)(2,1)} %param.4, f32[32,256]{1,0:T(8,128)S(1)} %gather_fusion.3, f32[32,256]{1,0:T(8,128)S(1)} %gather_fusion.2), kind=kLoop, calls=%fused_computation.21 | loop fusion | flops 12566528 | bytes 4325376 | tf_op jit(solution)/shard_map/reduce_max | solution.py:51
  75.2 0.8 scatter_custom_fusion.3
  76.0 0.7 broadcast_in_dim.13
  76.7 7.2 %all-to-all-start.1 = ((f32[16,16,256]{2,1,0:T(8,128)}), f32[16,16,256]{2,1,0:T(8,128)S(1)}, u32[]{:S(2)}, u32[]{:S(2)}) async-start(f32[16,16,256]{2,1,0:T(8,128)} %broadcast_in_dim.13), calls=%async_computation.1 | async-start | bytes 524288 | tf_op jit(solution)/shard_map/all_to_all | solution.py:20
  83.9 0.8 scatter_custom_fusion.2
  84.8 27.1 %pmax.44 = f32[32,256]{1,0:T(8,128)S(1)} all-reduce(f32[32,256]{1,0:T(8,128)S(1)} %scatter_custom_fusion.2), channel_id=1, replica_groups=mesh['prow'=16,'pcol_0'=8,'pcol_1'=4] {'pcol_0'}, use_global_device_ids=true, to_apply=%region_9.0 | all-reduce | flops 8192 | bytes 65536 | tf_op jit(solution)/shard_map/pmax | solution.py:14
  111.8 14.4 %pmax.45 = f32[32,256]{1,0:T(8,128)S(1)} all-reduce(f32[32,256]{1,0:T(8,128)S(1)} %pmax.44), channel_id=1, replica_groups=mesh['prow'=16,'pcol_0'=8,'pcol_1'=4] {'pcol_1'}, use_global_device_ids=true, to_apply=%region_10.0 | all-reduce | flops 8192 | bytes 65536 | tf_op jit(solution)/shard_map/pmax | solution.py:14
  126.3 0.6 gather_fusion.4
  126.9 0.0 all-to-all-done.1
  126.9 0.6 gather_fusion.5
  127.6 5.1 %fusion.3 = (f32[32,256]{1,0:T(8,128)S(1)}, f32[32,256]{1,0:T(8,128)S(1)}) fusion(bf16[1,1,32,256,256]{4,3,2,1,0:T(8,128)(2,1)} %param.4, f32[32,256]{1,0:T(8,128)S(1)} %gather_fusion.5, f32[32,256]{1,0:T(8,128)S(1)} %gather_fusion.4), kind=kLoop, calls=%fused_computation.19 | loop fusion | flops 12566528 | bytes 4325376 | tf_op jit(solution)/shard_map/reduce_max | solution.py:51
  132.7 0.8 scatter_custom_fusion.5
  133.5 0.7 broadcast_in_dim.14
  134.2 7.2 %all-to-all-start.2 = ((f32[16,16,256]{2,1,0:T(8,128)}), f32[16,16,256]{2,1,0:T(8,128)S(1)}, u32[]{:S(2)}, u32[]{:S(2)}) async-start(f32[16,16,256]{2,1,0:T(8,128)} %broadcast_in_dim.14), calls=%async_computation.2 | async-start | bytes 524288 | tf_op jit(solution)/shard_map/all_to_all | solution.py:20
  141.4 0.8 scatter_custom_fusion.4
  142.3 27.6 %pmax.46 = f32[32,256]{1,0:T(8,128)S(1)} all-reduce(f32[32,256]{1,0:T(8,128)S(1)} %scatter_custom_fusion.4), channel_id=1, replica_groups=mesh['prow'=16,'pcol_0'=8,'pcol_1'=4] {'pcol_0'}, use_global_device_ids=true, to_apply=%region_16.0 | all-reduce | flops 8192 | bytes 65536 | tf_op jit(solution)/shard_map/pmax | solution.py:14
  169.8 16.2 %pmax.47 = f32[32,256]{1,0:T(8,128)S(1)} all-reduce(f32[32,256]{1,0:T(8,128)S(1)} %pmax.46), channel_id=1, replica_groups=mesh['prow'=16,'pcol_0'=8,'pcol_1'=4] {'pcol_1'}, use_global_device_ids=true, to_apply=%region_17.0 | all-reduce | flops 8192 | bytes 65536 | tf_op jit(solution)/shard_map/pmax | solution.py:14
  186.1 0.6 copy.8
  186.7 0.0 all-to-all-done.2
  186.7 0.6 copy.9
  (14 shorter events, 0.2 us)
Async XLA Ops:
  10.5 58.9 %all-to-all-start = ((f32[16,16,256]{2,1,0:T(8,128)}), f32[16,16,256]{2,1,0:T(8,128)S(1)}, u32[]{:S(2)}, u32[]{:S(2)}) async-start(f32[16,16,256]{2,1,0:T(8,128)} %broadcast_in_dim.12), calls=%async_computation | async-start | bytes 524288 | tf_op jit(solution)/shard_map/all_to_all | solution.py:20
  76.7 50.2 %all-to-all-start.1 = ((f32[16,16,256]{2,1,0:T(8,128)}), f32[16,16,256]{2,1,0:T(8,128)S(1)}, u32[]{:S(2)}, u32[]{:S(2)}) async-start(f32[16,16,256]{2,1,0:T(8,128)} %broadcast_in_dim.13), calls=%async_computation.1 | async-start | bytes 524288 | tf_op jit(solution)/shard_map/all_to_all | solution.py:20
  134.2 52.5 %all-to-all-start.2 = ((f32[16,16,256]{2,1,0:T(8,128)}), f32[16,16,256]{2,1,0:T(8,128)S(1)}, u32[]{:S(2)}, u32[]{:S(2)}) async-start(f32[16,16,256]{2,1,0:T(8,128)} %broadcast_in_dim.14), calls=%async_computation.2 | async-start | bytes 524288 | tf_op jit(solution)/shard_map/all_to_all | solution.py:20
where the time goes:
time: 188 us; the launch traced here: 187 us
  blocking collectives  133 us (71%)
  starting transfers between devices  24.4 us (13%)
  other arithmetic  21.7 us (12%)
  local copies, waits for them, and re-layouts  7.07 us (4%)
    pmax x6, blocking collectives, one_axis_at_a_time(): value = lax.pmax(value, axis)  133 us
    all_to_all x3, starting transfers between devices, from_everyone(): lax.all_to_all(jnp.broadcast_to(value[None], (devices, *value.shape)), ax...  24.4 us
    reduce_max x2, other arithmetic, on_device(): col_part = jnp.max(scaled, axis=1) * alive[:, None]  10.2 us
    reduce_max x1, other arithmetic, on_device(): row_part = jnp.max(scaled, axis=2) * alive[:, None]  5.1 us
  transfers between devices with their start and end apart: 3, of which 0 were waited for; matrix products, arithmetic and copies ran while one was open for 2% of the time, Pallas kernels for 0%

commit v1 on v0

v1 whole, which is shorter than its diff:
```python
import functools

import jax
import jax.numpy as jnp
from jax import lax
from jax.experimental import pallas as pl
from jax.experimental.pallas import tpu as pltpu
from jax.sharding import Mesh
from jax.sharding import PartitionSpec as P

BR_DEV = 32
SWEEPS = 3
PER_COPY = 2
ROWS = 64


def sweep_body(weighted, count, brow, bcol, tiles, *refs):
    if weighted:
        row_scale, col_scale, row_out, col_out, held, turned, sems = refs
    else:
        row_out, col_out, held, sems = refs
    slots, width, _ = held.shape
    copies = slots // PER_COPY

    def fetch(k):
        part = pl.ds(k * PER_COPY, PER_COPY)
        return pltpu.make_async_copy(tiles.at[part], held.at[part], sems.at[k])

    for k in range(copies):
        fetch(k).start()
    row_out[...] = jnp.zeros(row_out.shape, jnp.float32)
    col_out[...] = jnp.zeros(col_out.shape, jnp.float32)
    if weighted:
        pad = jnp.zeros((128 - BR_DEV, width), jnp.float32)
        turned[...] = jnp.concatenate([row_scale[...], pad], axis=0).T
    lanes = lax.broadcasted_iota(jnp.int32, (ROWS, 128), 1)
    rows = lax.broadcasted_iota(jnp.int32, (ROWS, 128), 0)

    def one_tile(s):
        b = brow[s]
        c = bcol[s]
        col_max = None
        row_max = []
        if weighted:
            weight = col_scale[pl.ds(c, 1), :]
            here = lanes == b
        for h in range(0, width, ROWS):
            block = jnp.abs(held[s, pl.ds(h, ROWS), :])
            if weighted:
                own = turned[pl.ds(h, ROWS), :]
                scale = jnp.max(jnp.where(here, own, 0.0), axis=1, keepdims=True)
                block = block.astype(jnp.float32) * scale
                down = jnp.max(block.reshape(ROWS // 8, 8, width), axis=0)
                block = block * weight
                half = jnp.maximum(block[:, :128], block[:, 128:])
            else:
                down = jnp.max(block.reshape(ROWS // 16, 16, width), axis=0)
                half = jnp.maximum(block[:, :128], block[:, 128:]).astype(jnp.float32)
            col_max = down if col_max is None else jnp.maximum(col_max, down)
            across = jnp.max(half, axis=1, keepdims=True)
            placed = jnp.where(lanes == rows + h % 128, across, 0.0)
            placed = jnp.max(placed.reshape(ROWS // 8, 8, 128), axis=0)
            if h % 128:
                row_max[-1] = jnp.maximum(row_max[-1], placed)
            else:
                row_max.append(placed)
        live = s < count[0]
        col_max = jnp.max(col_max.astype(jnp.float32), axis=0, keepdims=True)
        row_max = jnp.concatenate([jnp.max(m, axis=0, keepdims=True) for m in row_max], axis=1)
        col_max = jnp.where(live, col_max, 0.0)
        row_max = jnp.where(live, row_max, 0.0)
        col_out[pl.ds(c, 1), :] = jnp.maximum(col_out[pl.ds(c, 1), :], col_max)
        row_out[pl.ds(b, 1), :] = jnp.maximum(row_out[pl.ds(b, 1), :], row_max)

    def step(k, carry):
        fetch(k).wait()

        @pl.when(k * PER_COPY < count[0])
        def _():
            for t in range(PER_COPY):
                one_tile(k * PER_COPY + t)

        return carry

    lax.fori_loop(0, copies, step, 0)


def sweep_call(tiles, brow, bcol, count, col_blocks, scales=None):
    slots, width, _ = tiles.shape
    smem = pl.BlockSpec(memory_space=pltpu.SMEM)
    vmem = pl.BlockSpec(memory_space=pltpu.VMEM)
    weighted = scales is not None
    scratch = [pltpu.VMEM((slots, width, width), tiles.dtype)]
    if weighted:
        scratch.append(pltpu.VMEM((width, 128), jnp.float32))
    scratch.append(pltpu.SemaphoreType.DMA((slots // PER_COPY,)))
    return pl.pallas_call(
        functools.partial(sweep_body, weighted),
        in_specs=[smem, smem, smem, pl.BlockSpec(memory_space=pltpu.HBM)] + [vmem] * (2 * weighted),
        out_specs=[vmem, vmem],
        out_shape=[
            jax.ShapeDtypeStruct((BR_DEV, width), jnp.float32),
            jax.ShapeDtypeStruct((col_blocks, width), jnp.float32),
        ],
        scratch_shapes=scratch,
        compiler_params=pltpu.CompilerParams(vmem_limit_bytes=16 * 2**20),
        name="weighted_sweep" if weighted else "first_sweep",
    )(count, brow, bcol, tiles, *(scales if weighted else ()))


PROW = ("z", "core")
PCOL = ("y4", "y2", "y1", "x2", "x1")


def from_everyone(value, axes):
    devices = lax.axis_size(axes)
    return lax.all_to_all(
        jnp.broadcast_to(value[None], (devices, *value.shape)), axes, 0, 0, tiled=True
    )


def with_partner(value, axis):
    both = lax.all_gather(value, axis, axis=0)
    return jnp.maximum(both[0], both[1])


def rescale(scale, largest):
    return scale / jnp.sqrt(largest)


def on_device(tiles, tile_brow, tile_bcol, tile_count):
    slots = tiles.shape[2]
    width = tiles.shape[3]
    col_blocks = BR_DEV * lax.axis_size(PROW) // lax.axis_size(PCOL)
    brow = tile_brow.reshape(slots)
    bcol = tile_bcol.reshape(slots)
    count = tile_count.reshape(1)
    block = tiles.reshape(slots, width, width)
    row_vec = col_vec = None
    for sweep in range(SWEEPS):
        scales = (row_vec, col_vec) if sweep else None
        row_max, col_max = sweep_call(block, brow, bcol, count, col_blocks, scales)
        col_max = with_partner(col_max, "core")
        col_max = from_everyone(col_max, "z")
        row_max = with_partner(row_max, "x1")
        row_max = with_partner(row_max, "y1")
        row_max = jnp.max(from_everyone(row_max, ("y4", "y2", "x2")), axis=0)
        col_max = jnp.max(col_max, axis=0)
        if sweep:
            row_vec = rescale(row_vec, row_max)
            col_vec = rescale(col_vec, col_vec * col_max)
        else:
            row_vec = 1.0 / jnp.sqrt(row_max)
            col_vec = 1.0 / jnp.sqrt(col_max)
    return (row_vec.reshape(BR_DEV, 1, width), col_vec.reshape(col_blocks, 1, width))


def solution(mesh):
    shape = (mesh.shape["prow"] // 2, 2, 2, 2, 2, 2, 2)
    finer = Mesh(mesh.devices.reshape(shape), PROW + PCOL)
    in_specs = (
        P(PROW, PCOL, None, None, None),
        P(PROW, PCOL, None),
        P(PROW, PCOL, None),
        P(PROW, PCOL),
    )
    out_specs = (P(None, PROW, None), P(None, PCOL, None))
    return jax.shard_map(
        on_device, mesh=finer, in_specs=in_specs, out_specs=out_specs, check_vma=False
    )
```

time: 188 us -> 139 us (0.74)
  the two profiles are of different devices: /device:TPU:64 before, /device:TPU:4 now
where the time goes in v1:
time: 139 us; the launch traced here: 138 us
  starting transfers between devices  45.8 us (33%)
  waiting for transfers between devices  36.8 us (26%)
  blocking collectives  32.9 us (24%)
  local copies, waits for them, and re-layouts  13.3 us (10%)
  Pallas kernels  7.59 us (5%)
  between operations  1.45 us (1%)
    all_to_all x6, starting transfers between devices, from_everyone(): lax.all_to_all(jnp.broadcast_to(value[None], (devices, *value.shape)), ax...  45.8 us
    all_to_all x6, waiting for transfers between devices, from_everyone(): lax.all_to_all(jnp.broadcast_to(value[None], (devices, *value.shape)), ax...  36.8 us
    all_gather x9, blocking collectives, with_partner(): both = lax.all_gather(value, axis, axis=0)  32.9 us
    unnamed x16, local copies, waits for them, and re-layouts  9.14 us
    pallas_call x3, Pallas kernels, sweep_call(): pl.pallas_call(functools.partial(sweep_body, weighted), in_specs=[smem, s...  7.59 us
    broadcast_in_dim x6, local copies, waits for them, and re-layouts, from_everyone(): jnp.broadcast_to(value[None], (devices, *value.shape))  4.13 us
  transfers between devices with their start and end apart: 6, of which 6 were waited for; matrix products, arithmetic and copies ran while one was open for 1% of the time, Pallas kernels for 0%

profile of v1, /device:TPU:4, one launch (start us, length us, event | category | flops | bytes accessed | tf_op | source)
XLA Modules:
  0.0 138.1 jit_solution(4647962790667739857)
XLA Ops:
  0.6 0.0 copy-start.4
  0.6 0.0 copy-start.6
  1.3 0.0 copy-start
  1.3 2.2 %copy-done = bf16[1,1,32,256,256]{4,3,2,1,0:T(8,128)(2,1)S(1)} copy-done((bf16[1,1,32,256,256]{4,3,2,1,0:T(8,128)(2,1)S(1)}, bf16[1,1,32,256,256]{4,3,2,1,0:T(8,128)(2,1)}, u32[]{:S(2)}) %copy-start) | copy-done | bytes 4194328
  3.5 0.0 copy-start.3
  3.5 0.7 copy-done.3
  4.2 0.0 copy-start.5
  4.2 0.7 copy-done.5
  4.8 2.1 %first_sweep.1 = (f32[32,256]{1,0:T(8,128)S(1)}, f32[16,256]{1,0:T(8,128)S(1)}) custom-call(s32[1]{0:T(128)} %bitcast.22.count, s32[32]{0:T(128)S(1)} %bitcast.28, s32[32]{0:T(128)S(1)} %bitcast.31, bf16[32,256,256]{2,1,0:T(8,128)(2,1)S(1)} %bitcast.25), custom_call_target="tpu_custom_call" | custom-call | tf_op jit(solution)/shard_map/first_sweep/pallas_call | solution.py:97
  6.9 1.8 %all-gather.1 = f32[32,256]{1,0:T(8,128)S(1)} all-gather(f32[16,256]{1,0:T(8,128)S(1)} %get-tuple-element.9), channel_id=3, replica_groups=mesh['z'=8,'core'=2,'y4'=2,'y2'=2,'y1'=2,'x2'=2,'x1'=2] {'core'}, dimensions={0}, use_global_device_ids=true | all-gather | bytes 49152 | tf_op jit(solution)/shard_map/all_gather | solution.py:123
  8.8 0.7 broadcast_in_dim.51
  9.4 10.6 %all-to-all-start.1 = ((f32[8,16,256]{2,1,0:T(8,128)}), f32[8,16,256]{2,1,0:T(8,128)S(1)}, u32[]{:S(2)}, u32[]{:S(2)}) async-start(f32[8,16,256]{2,1,0:T(8,128)} %broadcast_in_dim.51), calls=%async_computation.1 | async-start | bytes 262144 | tf_op jit(solution)/shard_map/all_to_all | solution.py:117
  20.0 4.6 %all-gather = f32[64,256]{1,0:T(8,128)S(1)} all-gather(f32[32,256]{1,0:T(8,128)S(1)} %get-tuple-element.8), channel_id=2, replica_groups=mesh['z'=8,'core'=2,'y4'=2,'y2'=2,'y1'=2,'x2'=2,'x1'=2] {'x1'}, dimensions={0}, use_global_device_ids=true | all-gather | bytes 98304 | tf_op jit(solution)/shard_map/all_gather | solution.py:123
  24.6 4.6 %all-gather.6 = f32[64,256]{1,0:T(8,128)S(1)} all-gather(f32[32,256]{1,0:T(8,128)S(1)} %slice_maximum_fusion.5), channel_id=8, replica_groups=mesh['z'=8,'core'=2,'y4'=2,'y2'=2,'y1'=2,'x2'=2,'x1'=2] {'y1'}, dimensions={0}, use_global_device_ids=true | all-gather | bytes 98304 | tf_op jit(solution)/shard_map/all_gather | solution.py:123
  29.2 0.2 all-to-all-done.1
  29.4 0.7 broadcast_in_dim.49
  30.2 10.1 %all-to-all-start = ((f32[8,32,256]{2,1,0:T(8,128)}), f32[8,32,256]{2,1,0:T(8,128)S(1)}, u32[]{:S(2)}, u32[]{:S(2)}) async-start(f32[8,32,256]{2,1,0:T(8,128)} %broadcast_in_dim.49), calls=%async_computation | async-start | bytes 524288 | tf_op jit(solution)/shard_map/all_to_all | solution.py:117
  40.2 9.1 %all-to-all-done = f32[8,32,256]{2,1,0:T(8,128)S(1)} async-done(((f32[8,32,256]{2,1,0:T(8,128)}), f32[8,32,256]{2,1,0:T(8,128)S(1)}, u32[]{:S(2)}, u32[]{:S(2)}) %all-to-all-start) | async-done | bytes 262176 | tf_op jit(solution)/shard_map/all_to_all | solution.py:117
  49.4 0.0 copy-done.4
  49.4 0.0 copy-done.6
  49.4 0.0 copy-start.1
  49.4 2.2 %copy-done.1 = bf16[1,1,32,256,256]{4,3,2,1,0:T(8,128)(2,1)S(1)} copy-done((bf16[1,1,32,256,256]{4,3,2,1,0:T(8,128)(2,1)S(1)}, bf16[1,1,32,256,256]{4,3,2,1,0:T(8,128)(2,1)}, u32[]{:S(2)}) %copy-start.1) | copy-done | bytes 4194328
  51.6 2.7 %weighted_sweep.2 = (f32[32,256]{1,0:T(8,128)S(1)}, f32[16,256]{1,0:T(8,128)S(1)}) custom-call(s32[1]{0:T(128)} %bitcast.23.count, s32[32]{0:T(128)S(1)} %bitcast.29, s32[32]{0:T(128)S(1)} %bitcast.32, bf16[32,256,256]{2,1,0:T(8,128)(2,1)S(1)} %bitcast.26, f32[32,256]{1,0:T(8,128)S(1)} %sqrt.22.refs_0_, f32[16,256]{1,0:T(8,128)S(1)} %sqrt.23.refs_1_), custom_call_target="tpu_custom_call" | custom-call | tf_op jit(solution)/shard_map/weighted_sweep/pallas_call | solution.py:97
  54.4 4.6 %all-gather.2 = f32[64,256]{1,0:T(8,128)S(1)} all-gather(f32[32,256]{1,0:T(8,128)S(1)} %get-tuple-element.10), channel_id=4, replica_groups=mesh['z'=8,'core'=2,'y4'=2,'y2'=2,'y1'=2,'x2'=2,'x1'=2] {'x1'}, dimensions={0}, use_global_device_ids=true | all-gather | bytes 98304 | tf_op jit(solution)/shard_map/all_gather | solution.py:123
  59.0 1.8 %all-gather.3 = f32[32,256]{1,0:T(8,128)S(1)} all-gather(f32[16,256]{1,0:T(8,128)S(1)} %get-tuple-element.11), channel_id=5, replica_groups=mesh['z'=8,'core'=2,'y4'=2,'y2'=2,'y1'=2,'x2'=2,'x1'=2] {'core'}, dimensions={0}, use_global_device_ids=true | all-gather | bytes 49152 | tf_op jit(solution)/shard_map/all_gather | solution.py:123
  60.8 0.7 broadcast_in_dim.55
  61.4 6.9 %all-to-all-start.3 = ((f32[8,16,256]{2,1,0:T(8,128)}), f32[8,16,256]{2,1,0:T(8,128)S(1)}, u32[]{:S(2)}, u32[]{:S(2)}) async-start(f32[8,16,256]{2,1,0:T(8,128)} %broadcast_in_dim.55), calls=%async_computation.3 | async-start | bytes 262144 | tf_op jit(solution)/shard_map/all_to_all | solution.py:117
  68.4 4.6 %all-gather.7 = f32[64,256]{1,0:T(8,128)S(1)} all-gather(f32[32,256]{1,0:T(8,128)S(1)} %slice_maximum_fusion.3), channel_id=9, replica_groups=mesh['z'=8,'core'=2,'y4'=2,'y2'=2,'y1'=2,'x2'=2,'x1'=2] {'y1'}, dimensions={0}, use_global_device_ids=true | all-gather | bytes 98304 | tf_op jit(solution)/shard_map/all_gather | solution.py:123
  73.0 4.8 %all-to-all-done.3 = f32[8,16,256]{2,1,0:T(8,128)S(1)} async-done(((f32[8,16,256]{2,1,0:T(8,128)}), f32[8,16,256]{2,1,0:T(8,128)S(1)}, u32[]{:S(2)}, u32[]{:S(2)}) %all-to-all-start.3) | async-done | bytes 131104 | tf_op jit(solution)/shard_map/all_to_all | solution.py:117
  77.8 0.7 broadcast_in_dim.53
  78.5 7.7 %all-to-all-start.2 = ((f32[8,32,256]{2,1,0:T(8,128)}), f32[8,32,256]{2,1,0:T(8,128)S(1)}, u32[]{:S(2)}, u32[]{:S(2)}) async-start(f32[8,32,256]{2,1,0:T(8,128)} %broadcast_in_dim.53), calls=%async_computation.2 | async-start | bytes 524288 | tf_op jit(solution)/shard_map/all_to_all | solution.py:117
  86.2 9.2 %all-to-all-done.2 = f32[8,32,256]{2,1,0:T(8,128)S(1)} async-done(((f32[8,32,256]{2,1,0:T(8,128)}), f32[8,32,256]{2,1,0:T(8,128)S(1)}, u32[]{:S(2)}, u32[]{:S(2)}) %all-to-all-start.2) | async-done | bytes 262176 | tf_op jit(solution)/shard_map/all_to_all | solution.py:117
  95.4 0.0 copy-start.2
  95.5 2.2 %copy-done.2 = bf16[1,1,32,256,256]{4,3,2,1,0:T(8,128)(2,1)S(1)} copy-done((bf16[1,1,32,256,256]{4,3,2,1,0:T(8,128)(2,1)S(1)}, bf16[1,1,32,256,256]{4,3,2,1,0:T(8,128)(2,1)}, u32[]{:S(2)}) %copy-start.2) | copy-done | bytes 4194328
  97.6 2.7 %weighted_sweep.3 = (f32[32,256]{1,0:T(8,128)S(1)}, f32[16,256]{1,0:T(8,128)S(1)}) custom-call(s32[1]{0:T(128)} %bitcast.24.count, s32[32]{0:T(128)S(1)} %bitcast.30, s32[32]{0:T(128)S(1)} %bitcast.33, bf16[32,256,256]{2,1,0:T(8,128)(2,1)S(1)} %bitcast.27, f32[32,256]{1,0:T(8,128)S(1)} %rsqrt_multiply_fusion.refs_0_, f32[16,256]{1,0:T(8,128)S(1)} %rsqrt_multiply_fusion.1.refs_1_), custom_call_target="tpu_custom_call" | custom-call | tf_op jit(solution)/shard_map/weighted_sweep/pallas_call | solution.py:97
  100.4 4.6 %all-gather.4 = f32[64,256]{1,0:T(8,128)S(1)} all-gather(f32[32,256]{1,0:T(8,128)S(1)} %get-tuple-element.12), channel_id=6, replica_groups=mesh['z'=8,'core'=2,'y4'=2,'y2'=2,'y1'=2,'x2'=2,'x1'=2] {'x1'}, dimensions={0}, use_global_device_ids=true | all-gather | bytes 98304 | tf_op jit(solution)/shard_map/all_gather | solution.py:123
  105.0 1.8 %all-gather.5 = f32[32,256]{1,0:T(8,128)S(1)} all-gather(f32[16,256]{1,0:T(8,128)S(1)} %get-tuple-element.13), channel_id=7, replica_groups=mesh['z'=8,'core'=2,'y4'=2,'y2'=2,'y1'=2,'x2'=2,'x1'=2] {'core'}, dimensions={0}, use_global_device_ids=true | all-gather | bytes 49152 | tf_op jit(solution)/shard_map/all_gather | solution.py:123
  106.8 0.7 broadcast_in_dim.59
  107.5 4.3 %all-to-all-start.5 = ((f32[8,16,256]{2,1,0:T(8,128)}), f32[8,16,256]{2,1,0:T(8,128)S(1)}, u32[]{:S(2)}, u32[]{:S(2)}) async-start(f32[8,16,256]{2,1,0:T(8,128)} %broadcast_in_dim.59), calls=%async_computation.5 | async-start | bytes 262144 | tf_op jit(solution)/shard_map/all_to_all | solution.py:117
  111.7 4.6 %all-gather.8 = f32[64,256]{1,0:T(8,128)S(1)} all-gather(f32[32,256]{1,0:T(8,128)S(1)} %slice_maximum_fusion.1), channel_id=10, replica_groups=mesh['z'=8,'core'=2,'y4'=2,'y2'=2,'y1'=2,'x2'=2,'x1'=2] {'y1'}, dimensions={0}, use_global_device_ids=true | all-gather | bytes 98304 | tf_op jit(solution)/shard_map/all_gather | solution.py:123
  116.3 4.8 %all-to-all-done.5 = f32[8,16,256]{2,1,0:T(8,128)S(1)} async-done(((f32[8,16,256]{2,1,0:T(8,128)}), f32[8,16,256]{2,1,0:T(8,128)S(1)}, u32[]{:S(2)}, u32[]{:S(2)}) %all-to-all-start.5) | async-done | bytes 131104 | tf_op jit(solution)/shard_map/all_to_all | solution.py:117
  121.1 0.7 broadcast_in_dim.57
  121.8 6.3 %all-to-all-start.4 = ((f32[8,32,256]{2,1,0:T(8,128)}), f32[8,32,256]{2,1,0:T(8,128)S(1)}, u32[]{:S(2)}, u32[]{:S(2)}) async-start(f32[8,32,256]{2,1,0:T(8,128)} %broadcast_in_dim.57), calls=%async_computation.4 | async-start | bytes 524288 | tf_op jit(solution)/shard_map/all_to_all | solution.py:117
  128.1 0.6 copy.9
  128.8 8.6 %all-to-all-done.4 = f32[8,32,256]{2,1,0:T(8,128)S(1)} async-done(((f32[8,32,256]{2,1,0:T(8,128)}), f32[8,32,256]{2,1,0:T(8,128)S(1)}, u32[]{:S(2)}, u32[]{:S(2)}) %all-to-all-start.4) | async-done | bytes 262176 | tf_op jit(solution)/shard_map/all_to_all | solution.py:117
  137.4 0.6 copy.8
  (21 shorter events, 0.2 us)
Async XLA Ops:
  0.6 48.8 %copy-start.4 = (s32[1,1,32]{2,1,0:T(1,128)S(1)}, s32[1,1,32]{2,1,0:T(1,128)}, u32[]{:S(2)}) copy-start(s32[1,1,32]{2,1,0:T(1,128)} %param.5) | copy-start | bytes 388
  0.6 48.8 %copy-start.6 = (s32[1,1,32]{2,1,0:T(1,128)S(1)}, s32[1,1,32]{2,1,0:T(1,128)}, u32[]{:S(2)}) copy-start(s32[1,1,32]{2,1,0:T(1,128)} %param.6) | copy-start | bytes 388
  1.3 2.2 %copy-start = (bf16[1,1,32,256,256]{4,3,2,1,0:T(8,128)(2,1)S(1)}, bf16[1,1,32,256,256]{4,3,2,1,0:T(8,128)(2,1)}, u32[]{:S(2)}) copy-start(bf16[1,1,32,256,256]{4,3,2,1,0:T(8,128)(2,1)} %param.4) | copy-start | bytes 12582916
  3.5 0.7 copy-start.3
  4.2 0.7 copy-start.5
  9.4 20.0 %all-to-all-start.1 = ((f32[8,16,256]{2,1,0:T(8,128)}), f32[8,16,256]{2,1,0:T(8,128)S(1)}, u32[]{:S(2)}, u32[]{:S(2)}) async-start(f32[8,16,256]{2,1,0:T(8,128)} %broadcast_in_dim.51), calls=%async_computation.1 | async-start | bytes 262144 | tf_op jit(solution)/shard_map/all_to_all | solution.py:117
  30.2 19.2 %all-to-all-start = ((f32[8,32,256]{2,1,0:T(8,128)}), f32[8,32,256]{2,1,0:T(8,128)S(1)}, u32[]{:S(2)}, u32[]{:S(2)}) async-start(f32[8,32,256]{2,1,0:T(8,128)} %broadcast_in_dim.49), calls=%async_computation | async-start | bytes 524288 | tf_op jit(solution)/shard_map/all_to_all | solution.py:117
  49.4 2.2 %copy-start.1 = (bf16[1,1,32,256,256]{4,3,2,1,0:T(8,128)(2,1)S(1)}, bf16[1,1,32,256,256]{4,3,2,1,0:T(8,128)(2,1)}, u32[]{:S(2)}) copy-start(bf16[1,1,32,256,256]{4,3,2,1,0:T(8,128)(2,1)} %param.4) | copy-start | bytes 12582916
  61.4 16.3 %all-to-all-start.3 = ((f32[8,16,256]{2,1,0:T(8,128)}), f32[8,16,256]{2,1,0:T(8,128)S(1)}, u32[]{:S(2)}, u32[]{:S(2)}) async-start(f32[8,16,256]{2,1,0:T(8,128)} %broadcast_in_dim.55), calls=%async_computation.3 | async-start | bytes 262144 | tf_op jit(solution)/shard_map/all_to_all | solution.py:117
  78.5 16.9 %all-to-all-start.2 = ((f32[8,32,256]{2,1,0:T(8,128)}), f32[8,32,256]{2,1,0:T(8,128)S(1)}, u32[]{:S(2)}, u32[]{:S(2)}) async-start(f32[8,32,256]{2,1,0:T(8,128)} %broadcast_in_dim.53), calls=%async_computation.2 | async-start | bytes 524288 | tf_op jit(solution)/shard_map/all_to_all | solution.py:117
  95.4 2.2 %copy-start.2 = (bf16[1,1,32,256,256]{4,3,2,1,0:T(8,128)(2,1)S(1)}, bf16[1,1,32,256,256]{4,3,2,1,0:T(8,128)(2,1)}, u32[]{:S(2)}) copy-start(bf16[1,1,32,256,256]{4,3,2,1,0:T(8,128)(2,1)} %param.4) | copy-start | bytes 12582916
  107.5 13.6 %all-to-all-start.5 = ((f32[8,16,256]{2,1,0:T(8,128)}), f32[8,16,256]{2,1,0:T(8,128)S(1)}, u32[]{:S(2)}, u32[]{:S(2)}) async-start(f32[8,16,256]{2,1,0:T(8,128)} %broadcast_in_dim.59), calls=%async_computation.5 | async-start | bytes 262144 | tf_op jit(solution)/shard_map/all_to_all | solution.py:117
  121.8 15.6 %all-to-all-start.4 = ((f32[8,32,256]{2,1,0:T(8,128)}), f32[8,32,256]{2,1,0:T(8,128)S(1)}, u32[]{:S(2)}, u32[]{:S(2)}) async-start(f32[8,32,256]{2,1,0:T(8,128)} %broadcast_in_dim.57), calls=%async_computation.4 | async-start | bytes 524288 | tf_op jit(solution)/shard_map/all_to_all | solution.py:117

commit v2 on v1

v2 whole, which is shorter than its diff:
```python
import functools

import jax
import jax.numpy as jnp
from jax import lax
from jax.experimental import pallas as pl
from jax.experimental.pallas import tpu as pltpu
from jax.sharding import Mesh
from jax.sharding import PartitionSpec as P

BR_DEV = 32
SWEEPS = 3
PER_COPY = 2
ROWS = 64
LANES = 128
VMEM = 52 * 2**20


def sweep_body(weighted, count_in, brow_in, bcol_in, tiles, *refs):
    if weighted:
        row_scale, col_scale, *refs = refs
    row_out, col_out, count, brow, bcol, held, sems, folded_a, folded_b, *refs = refs
    folded = (folded_a, folded_b)
    if weighted:
        spread, *turned = refs
    slots, width, _ = held.shape
    copies = slots // PER_COPY

    def fetch(k):
        part = pl.ds(k * PER_COPY, PER_COPY)
        return pltpu.make_async_copy(tiles.at[part], held.at[part], sems.at[k])

    small = [
        pltpu.make_async_copy(src, dst, sems.at[copies + i])
        for i, (src, dst) in enumerate(((count_in, count), (brow_in, brow), (bcol_in, bcol)))
    ]
    for copy in small:
        copy.start()
    for k in range(copies):
        fetch(k).start()
    row_out[...] = jnp.zeros(row_out.shape, jnp.float32)
    col_out[...] = jnp.zeros(col_out.shape, jnp.float32)
    if weighted:
        left = row_scale[...]
        parts = []
        for _ in range(3):
            parts.append(left.astype(jnp.bfloat16).astype(jnp.float32))
            left = left - parts[-1]
        parts.append(jnp.zeros((LANES - 3 * BR_DEV, width), jnp.float32))
        spread[...] = jnp.concatenate(parts, axis=0).T.astype(jnp.bfloat16)
    lane = lax.broadcasted_iota(jnp.int32, (ROWS, LANES), 1)
    row = lax.broadcasted_iota(jnp.int32, (ROWS, LANES), 0)
    for copy in small:
        copy.wait()
    live_slots = count[0, 0]

    def turn(s, out):
        part = lax.broadcasted_iota(jnp.int32, (LANES, LANES), 0)
        pick = (part % BR_DEV == brow[0, 0, s]) & (part < 3 * BR_DEV)
        pick = jnp.where(pick, 1.0, 0.0).astype(jnp.bfloat16)
        out[...] = jnp.dot(spread[...], pick, preferred_element_type=jnp.float32)

    def fold(s, scale, out):
        c = bcol[0, 0, s]
        if weighted:
            weight = col_scale[pl.ds(c, 1), :]
        tops = [None, None]
        for h in range(0, width, ROWS):
            block = jnp.abs(held[s, pl.ds(h, ROWS), :])
            best = None
            for side in range(2):
                x = block[:, side * LANES : (side + 1) * LANES]
                group = 16
                if weighted:
                    x = x.astype(jnp.float32) * scale[pl.ds(h, ROWS), :]
                    group = 8
                down = jnp.max(x.reshape(ROWS // group, group, LANES), axis=0)
                tops[side] = down if tops[side] is None else jnp.maximum(tops[side], down)
                if weighted:
                    x = x * weight[:, side * LANES : (side + 1) * LANES]
                best = x if best is None else jnp.maximum(best, x)
            out[pl.ds(h, ROWS), :] = best.astype(jnp.float32)
        top = jnp.concatenate(
            [jnp.max(t.astype(jnp.float32), axis=0, keepdims=True) for t in tops], axis=1
        )
        top = jnp.where(s < live_slots, top, 0.0)
        col_out[pl.ds(c, 1), :] = jnp.maximum(col_out[pl.ds(c, 1), :], top)

    def gather(s, source):
        b = brow[0, 0, jnp.maximum(s, 0)]
        sides = []
        for h in range(0, width, ROWS):
            across = jnp.max(source[pl.ds(h, ROWS), :], axis=1, keepdims=True)
            placed = jnp.where(lane == row + h % LANES, across, 0.0)
            placed = jnp.max(placed.reshape(ROWS // 8, 8, LANES), axis=0)
            if h % LANES:
                sides[-1] = jnp.maximum(sides[-1], placed)
            else:
                sides.append(placed)
        best = jnp.concatenate([jnp.max(p, axis=0, keepdims=True) for p in sides], axis=1)
        best = jnp.where((s >= 0) & (s < live_slots), best, 0.0)
        row_out[pl.ds(b, 1), :] = jnp.maximum(row_out[pl.ds(b, 1), :], best)

    if weighted:
        for t in range(PER_COPY):
            turn(t, turned[0].at[t])

    def step(k, carry):
        for odd in range(2):
            fetch(2 * k + odd).wait()
        for odd in range(2):
            for t in range(PER_COPY):
                s = (2 * k + odd) * PER_COPY + t
                if weighted:
                    turn(jnp.minimum(s + PER_COPY, slots - 1), turned[1 - odd].at[t])
                fold(s, turned[odd].at[t] if weighted else None, folded[odd].at[t])
                gather(s - PER_COPY, folded[1 - odd].at[t])
        return carry

    steps = (live_slots + 2 * PER_COPY - 1) // (2 * PER_COPY)
    lax.fori_loop(0, steps, step, 0)
    for t in range(PER_COPY):
        gather(steps * 2 * PER_COPY - PER_COPY + t, folded[1].at[t])

    def rest(k, carry):
        fetch(k).wait()
        return carry

    lax.fori_loop(2 * steps, copies, rest, 0)


def sweep_call(tiles, brow, bcol, count, col_blocks, scales=None):
    slots, width, _ = tiles.shape
    hbm = pl.BlockSpec(memory_space=pltpu.HBM)
    vmem = pl.BlockSpec(memory_space=pltpu.VMEM)
    weighted = scales is not None
    pair = pltpu.VMEM((PER_COPY, width, LANES), jnp.float32)
    scratch = [pltpu.SMEM(x.shape, x.dtype) for x in (count, brow, bcol)]
    scratch.append(pltpu.VMEM((slots, width, width), tiles.dtype))
    scratch.append(pltpu.SemaphoreType.DMA((slots // PER_COPY + 3,)))
    scratch += [pair, pair]
    if weighted:
        scratch += [pltpu.VMEM((width, LANES), jnp.bfloat16), pair, pair]
    return pl.pallas_call(
        functools.partial(sweep_body, weighted),
        in_specs=[hbm] * 4 + [vmem] * (2 * weighted),
        out_specs=[vmem, vmem],
        out_shape=[
            jax.ShapeDtypeStruct((BR_DEV, width), jnp.float32),
            jax.ShapeDtypeStruct((col_blocks, width), jnp.float32),
        ],
        scratch_shapes=scratch,
        compiler_params=pltpu.CompilerParams(vmem_limit_bytes=VMEM),
        name="weighted_sweep" if weighted else "first_sweep",
    )(count, brow, bcol, tiles, *(scales if weighted else ()))


PROW = ("z", "core")
PCOL = ("y4", "y2", "y1", "x2", "x1")


def from_everyone(value, axes):
    devices = lax.axis_size(axes)
    return lax.all_to_all(
        jnp.broadcast_to(value[None], (devices, *value.shape)), axes, 0, 0, tiled=True
    )


def with_partner(value, axis):
    both = lax.all_gather(value, axis, axis=0)
    return jnp.maximum(both[0], both[1])


def rescale(scale, largest):
    return scale / jnp.sqrt(largest)


def on_device(tiles, tile_brow, tile_bcol, tile_count):
    slots = tiles.shape[2]
    width = tiles.shape[3]
    col_blocks = BR_DEV * lax.axis_size(PROW) // lax.axis_size(PCOL)
    block = tiles.reshape(slots, width, width)
    row_vec = col_vec = None
    for sweep in range(SWEEPS):
        scales = (row_vec, col_vec) if sweep else None
        row_max, col_max = sweep_call(block, tile_brow, tile_bcol, tile_count, col_blocks, scales)
        row_max = jnp.max(from_everyone(row_max, ("x2", "x1", "y1",)), axis=0)
        row_max, col_max = lax.optimization_barrier((row_max, col_max))
        col_max = from_everyone(col_max, PROW)
        row_max = with_partner(row_max, "y4")
        row_max = with_partner(row_max, "y2")
        row_max, col_max = lax.optimization_barrier((row_max, col_max))
        col_max = jnp.max(col_max, axis=0)
        if sweep:
            row_vec = rescale(row_vec, row_max)
            col_vec = rescale(col_vec, col_vec * col_max)
        else:
            row_vec = 1.0 / jnp.sqrt(row_max)
            col_vec = 1.0 / jnp.sqrt(col_max)
    return (row_vec.reshape(BR_DEV, 1, width), col_vec.reshape(col_blocks, 1, width))


def solution(mesh):
    shape = (mesh.shape["prow"] // 2, 2, 2, 2, 2, 2, 2)
    finer = Mesh(mesh.devices.reshape(shape), PROW + PCOL)
    in_specs = (
        P(PROW, PCOL, None, None, None),
        P(PROW, PCOL, None),
        P(PROW, PCOL, None),
        P(PROW, PCOL),
    )
    out_specs = (P(None, PROW, None), P(None, PCOL, None))
    return jax.shard_map(
        on_device, mesh=finer, in_specs=in_specs, out_specs=out_specs, check_vma=False
    )
```

time: 139 us -> 117 us (0.84)
  the two profiles are of different devices: /device:TPU:4 before, /device:TPU:16 now
where the time goes in v2:
time: 117 us; the launch traced here: 116 us
  blocking collectives  74.7 us (64%)
  starting transfers between devices  28 us (24%)
  Pallas kernels  6.92 us (6%)
  local copies, waits for them, and re-layouts  4.82 us (4%)
  between operations  1.5 us (1%)
    all_gather x6, blocking collectives, with_partner(): both = lax.all_gather(value, axis, axis=0)  42 us
    all_to_all x3, blocking collectives, from_everyone(): lax.all_to_all(jnp.broadcast_to(value[None], (devices, *value.shape)), ax...  32.8 us
    all_to_all x3, starting transfers between devices, from_everyone(): lax.all_to_all(jnp.broadcast_to(value[None], (devices, *value.shape)), ax...  28 us
    pallas_call x3, Pallas kernels, sweep_call(): pl.pallas_call(functools.partial(sweep_body, weighted), in_specs=[hbm] *...  6.92 us
    unnamed x10, local copies, waits for them, and re-layouts  2.59 us
  transfers between devices with their start and end apart: 3, of which 0 were waited for; matrix products, arithmetic and copies ran while one was open for 0% of the time, Pallas kernels for 0%

profile of v2, /device:TPU:16, one launch (start us, length us, event | category | flops | bytes accessed | tf_op | source)
XLA Modules:
  0.0 116.2 jit_solution(14963500918140032618)
XLA Ops:
  0.6 0.0 copy-start.3
  0.6 0.0 copy-start.1
  1.3 0.0 copy-start
  1.3 0.6 copy-done
  2.0 0.0 copy-start.2
  2.0 0.7 copy-done.2
  2.6 2.3 %first_sweep.1 = (f32[32,256]{1,0:T(8,128)S(1)}, f32[16,256]{1,0:T(8,128)S(1)}) custom-call(s32[1,1]{1,0:T(1,128)S(6)} %copy.10.count_in, s32[1,1,32]{2,1,0:T(1,128)S(1)} %copy-done, s32[1,1,32]{2,1,0:T(1,128)S(1)} %copy-done.2, bf16[32,256,256]{2,1,0:T(8,128)(2,1)} %bitcast.19), custom_call_target="tpu_custom_call" | custom-call | tf_op jit(solution)/shard_map/first_sweep/pallas_call | solution.py:144
  5.0 12.5 %all_to_all.30 = f32[8,32,256]{2,1,0:T(8,128)S(1)} all-to-all(f32[8,32,256]{2,1,0:T(8,128)S(1)} %broadcast_in_dim.12), channel_id=1, replica_groups=mesh['z'=8,'core'=2,'y4'=2,'y2'=2,'y1'=2,'x2'=2,'x1'=2] {'x2','x1','y1'}, dimensions={0} | all-to-all | bytes 524288 | tf_op jit(solution)/shard_map/all_to_all | solution.py:164
  17.5 0.7 broadcast_in_dim.13
  18.2 11.4 %all-to-all-start.1 = ((f32[16,16,256]{2,1,0:T(8,128)}), f32[16,16,256]{2,1,0:T(8,128)S(1)}, u32[]{:S(2)}, u32[]{:S(2)}) async-start(f32[16,16,256]{2,1,0:T(8,128)} %broadcast_in_dim.13), calls=%async_computation.1 | async-start | bytes 524288 | tf_op jit(solution)/shard_map/all_to_all | solution.py:164
  29.7 8.5 %all-gather = f32[64,256]{1,0:T(8,128)S(1)} all-gather(f32[32,256]{1,0:T(8,128)S(1)} %reduce_max.58), channel_id=2, replica_groups=mesh['z'=8,'core'=2,'y4'=2,'y2'=2,'y1'=2,'x2'=2,'x1'=2] {'y4'}, dimensions={0}, use_global_device_ids=true | all-gather | bytes 98304 | tf_op jit(solution)/shard_map/all_gather | solution.py:170
  38.2 5.5 %all-gather.3 = f32[64,256]{1,0:T(8,128)S(1)} all-gather(f32[32,256]{1,0:T(8,128)S(1)} %slice_maximum_fusion.5), channel_id=5, replica_groups=mesh['z'=8,'core'=2,'y4'=2,'y2'=2,'y1'=2,'x2'=2,'x1'=2] {'y2'}, dimensions={0}, use_global_device_ids=true | all-gather | bytes 98304 | tf_op jit(solution)/shard_map/all_gather | solution.py:170
  43.7 0.0 all-to-all-done.1
  43.7 0.0 copy-done.3
  43.8 0.0 copy-done.1
  43.8 2.3 %weighted_sweep.2 = (f32[32,256]{1,0:T(8,128)S(1)}, f32[16,256]{1,0:T(8,128)S(1)}) custom-call(s32[1,1]{1,0:T(1,128)S(6)} %copy.10.count_in, s32[1,1,32]{2,1,0:T(1,128)S(1)} %copy-done.1, s32[1,1,32]{2,1,0:T(1,128)S(1)} %copy-done.3, bf16[32,256,256]{2,1,0:T(8,128)(2,1)} %bitcast.20, f32[32,256]{1,0:T(8,128)S(1)} %sqrt.22.refs_0_, f32[16,256]{1,0:T(8,128)S(1)} %sqrt.23.refs_1_), custom_call_target="tpu_custom_call" | custom-call | tf_op jit(solution)/shard_map/weighted_sweep/pallas_call | solution.py:144
  46.1 9.8 %all_to_all.31 = f32[8,32,256]{2,1,0:T(8,128)S(1)} all-to-all(f32[8,32,256]{2,1,0:T(8,128)S(1)} %broadcast_in_dim.14), channel_id=1, replica_groups=mesh['z'=8,'core'=2,'y4'=2,'y2'=2,'y1'=2,'x2'=2,'x1'=2] {'x2','x1','y1'}, dimensions={0} | all-to-all | bytes 524288 | tf_op jit(solution)/shard_map/all_to_all | solution.py:164
  56.0 0.7 broadcast_in_dim.15
  56.7 8.5 %all-to-all-start.3 = ((f32[16,16,256]{2,1,0:T(8,128)}), f32[16,16,256]{2,1,0:T(8,128)S(1)}, u32[]{:S(2)}, u32[]{:S(2)}) async-start(f32[16,16,256]{2,1,0:T(8,128)} %broadcast_in_dim.15), calls=%async_computation.3 | async-start | bytes 524288 | tf_op jit(solution)/shard_map/all_to_all | solution.py:164
  65.2 8.5 %all-gather.1 = f32[64,256]{1,0:T(8,128)S(1)} all-gather(f32[32,256]{1,0:T(8,128)S(1)} %reduce_max.60), channel_id=3, replica_groups=mesh['z'=8,'core'=2,'y4'=2,'y2'=2,'y1'=2,'x2'=2,'x1'=2] {'y4'}, dimensions={0}, use_global_device_ids=true | all-gather | bytes 98304 | tf_op jit(solution)/shard_map/all_gather | solution.py:170
  73.7 5.6 %all-gather.4 = f32[64,256]{1,0:T(8,128)S(1)} all-gather(f32[32,256]{1,0:T(8,128)S(1)} %slice_maximum_fusion.3), channel_id=6, replica_groups=mesh['z'=8,'core'=2,'y4'=2,'y2'=2,'y1'=2,'x2'=2,'x1'=2] {'y2'}, dimensions={0}, use_global_device_ids=true | all-gather | bytes 98304 | tf_op jit(solution)/shard_map/all_gather | solution.py:170
  79.3 0.0 all-to-all-done.3
  79.4 2.3 %weighted_sweep.3 = (f32[32,256]{1,0:T(8,128)S(1)}, f32[16,256]{1,0:T(8,128)S(1)}) custom-call(s32[1,1]{1,0:T(1,128)S(6)} %copy.10.count_in, s32[1,1,32]{2,1,0:T(1,128)S(1)} %copy-done.1, s32[1,1,32]{2,1,0:T(1,128)S(1)} %copy-done.3, bf16[32,256,256]{2,1,0:T(8,128)(2,1)} %bitcast.21, f32[32,256]{1,0:T(8,128)S(1)} %rsqrt_multiply_fusion.refs_0_, ...), custom_call_target="tpu_custom_call" | custom-call | tf_op jit(solution)/shard_map/weighted_sweep/pallas_call | solution.py:144
  81.7 10.4 %all_to_all.32 = f32[8,32,256]{2,1,0:T(8,128)S(1)} all-to-all(f32[8,32,256]{2,1,0:T(8,128)S(1)} %broadcast_in_dim.16), channel_id=1, replica_groups=mesh['z'=8,'core'=2,'y4'=2,'y2'=2,'y1'=2,'x2'=2,'x1'=2] {'x2','x1','y1'}, dimensions={0} | all-to-all | bytes 524288 | tf_op jit(solution)/shard_map/all_to_all | solution.py:164
  92.1 0.7 broadcast_in_dim.17
  92.9 8.0 %all-to-all-start.5 = ((f32[16,16,256]{2,1,0:T(8,128)}), f32[16,16,256]{2,1,0:T(8,128)S(1)}, u32[]{:S(2)}, u32[]{:S(2)}) async-start(f32[16,16,256]{2,1,0:T(8,128)} %broadcast_in_dim.17), calls=%async_computation.5 | async-start | bytes 524288 | tf_op jit(solution)/shard_map/all_to_all | solution.py:164
  100.9 8.5 %all-gather.2 = f32[64,256]{1,0:T(8,128)S(1)} all-gather(f32[32,256]{1,0:T(8,128)S(1)} %reduce_max.62), channel_id=4, replica_groups=mesh['z'=8,'core'=2,'y4'=2,'y2'=2,'y1'=2,'x2'=2,'x1'=2] {'y4'}, dimensions={0}, use_global_device_ids=true | all-gather | bytes 98304 | tf_op jit(solution)/shard_map/all_gather | solution.py:170
  109.4 5.5 %all-gather.5 = f32[64,256]{1,0:T(8,128)S(1)} all-gather(f32[32,256]{1,0:T(8,128)S(1)} %slice_maximum_fusion.1), channel_id=7, replica_groups=mesh['z'=8,'core'=2,'y4'=2,'y2'=2,'y1'=2,'x2'=2,'x1'=2] {'y2'}, dimensions={0}, use_global_device_ids=true | all-gather | bytes 98304 | tf_op jit(solution)/shard_map/all_gather | solution.py:170
  114.8 0.0 all-to-all-done.5
  114.9 0.6 copy.8
  115.6 0.6 copy.9
  (21 shorter events, 0.3 us)
Async XLA Ops:
  0.6 43.1 %copy-start.3 = (s32[1,1,32]{2,1,0:T(1,128)S(1)}, s32[1,1,32]{2,1,0:T(1,128)}, u32[]{:S(2)}) copy-start(s32[1,1,32]{2,1,0:T(1,128)} %bcol_in.5) | copy-start | bytes 388
  0.6 43.1 %copy-start.1 = (s32[1,1,32]{2,1,0:T(1,128)S(1)}, s32[1,1,32]{2,1,0:T(1,128)}, u32[]{:S(2)}) copy-start(s32[1,1,32]{2,1,0:T(1,128)} %brow_in.5) | copy-start | bytes 388
  1.3 0.7 copy-start
  2.0 0.7 copy-start.2
  18.2 25.4 %all-to-all-start.1 = ((f32[16,16,256]{2,1,0:T(8,128)}), f32[16,16,256]{2,1,0:T(8,128)S(1)}, u32[]{:S(2)}, u32[]{:S(2)}) async-start(f32[16,16,256]{2,1,0:T(8,128)} %broadcast_in_dim.13), calls=%async_computation.1 | async-start | bytes 524288 | tf_op jit(solution)/shard_map/all_to_all | solution.py:164
  56.7 22.6 %all-to-all-start.3 = ((f32[16,16,256]{2,1,0:T(8,128)}), f32[16,16,256]{2,1,0:T(8,128)S(1)}, u32[]{:S(2)}, u32[]{:S(2)}) async-start(f32[16,16,256]{2,1,0:T(8,128)} %broadcast_in_dim.15), calls=%async_computation.3 | async-start | bytes 524288 | tf_op jit(solution)/shard_map/all_to_all | solution.py:164
  92.9 22.0 %all-to-all-start.5 = ((f32[16,16,256]{2,1,0:T(8,128)}), f32[16,16,256]{2,1,0:T(8,128)S(1)}, u32[]{:S(2)}, u32[]{:S(2)}) async-start(f32[16,16,256]{2,1,0:T(8,128)} %broadcast_in_dim.17), calls=%async_computation.5 | async-start | bytes 524288 | tf_op jit(solution)/shard_map/all_to_all | solution.py:164

commit v3 on v2

v3 whole, which is shorter than its diff:
```python
import functools

import jax
import jax.numpy as jnp
from jax import lax
from jax.experimental import pallas as pl
from jax.experimental.pallas import tpu as pltpu
from jax.sharding import Mesh
from jax.sharding import PartitionSpec as P

BR_DEV = 32
SWEEPS = 3
PER_COPY = 2
ROWS = 64
KEPT = 12
FOLD1 = jnp.float32
LANES = 128
VMEM = 52 * 2**20


def sweep_body(weighted, meta_in, tiles, *refs):
    if weighted:
        kept, row_scale, col_scale, row_out, col_out, *refs = refs
    else:
        row_out, col_out, kept, *refs = refs
    meta, held, sems, folded_a, folded_b, *refs = refs
    folded = (folded_a, folded_b)
    if weighted:
        spread, *turned = refs
    first = kept.shape[0]
    width = kept.shape[1]
    slots = first + held.shape[0]
    copies = slots // PER_COPY
    own = first // PER_COPY

    def fetch(k, target, base):
        part = pl.ds(k * PER_COPY, PER_COPY)
        to = pl.ds((k - base) * PER_COPY, PER_COPY)
        return pltpu.make_async_copy(tiles.at[part], target.at[to], sems.at[k])

    about = pltpu.make_async_copy(meta_in, meta, sems.at[copies])
    about.start()
    if not weighted:
        for k in range(own):
            fetch(k, kept, 0).start()
        for k in range(own, copies):
            fetch(k, held, own).start()
    row_out[...] = jnp.zeros(row_out.shape, jnp.float32)
    col_out[...] = jnp.zeros(col_out.shape, jnp.float32)
    about.wait()
    live_slots = meta[0, 2 * slots]
    fetched = copies
    if weighted:
        fetched = jnp.where(live_slots > first, copies, own)

        def get(k, carry):
            fetch(k, held, own).start()
            return carry

        lax.fori_loop(own, fetched, get, 0)
        left = row_scale[...]
        parts = []
        for _ in range(3):
            parts.append(left.astype(jnp.bfloat16).astype(jnp.float32))
            left = left - parts[-1]
        parts.append(jnp.zeros((LANES - 3 * BR_DEV, width), jnp.float32))
        spread[...] = jnp.concatenate(parts, axis=0).T.astype(jnp.bfloat16)

    def turn(s, out):
        part = lax.broadcasted_iota(jnp.int32, (LANES, LANES), 0)
        pick = jnp.where(part % BR_DEV == meta[0, s], 1.0, 0.0).astype(jnp.bfloat16)
        out[...] = jnp.dot(spread[...], pick, preferred_element_type=jnp.float32)

    def fold(s, block_of, scale, out):
        c = meta[0, slots + s]
        if weighted:
            weight = col_scale[pl.ds(c, 1), :]
        tops = [None, None]
        for h in range(0, width, ROWS):
            block = jnp.abs(block_of[pl.ds(h, ROWS), :])
            best = None
            for side in range(2):
                x = block[:, side * LANES : (side + 1) * LANES]
                group = 16
                if weighted:
                    x = x.astype(jnp.float32) * scale[pl.ds(h, ROWS), :]
                    group = 8
                down = jnp.max(x.reshape(ROWS // group, group, LANES), axis=0)
                tops[side] = down if tops[side] is None else jnp.maximum(tops[side], down)
                if weighted:
                    x = x * weight[:, side * LANES : (side + 1) * LANES]
                best = x if best is None else jnp.maximum(best, x)
            out[pl.ds(h, ROWS), :] = best.astype(out.dtype)
        top = jnp.concatenate(
            [jnp.max(t.astype(jnp.float32), axis=0, keepdims=True) for t in tops], axis=1
        )
        top = jnp.where(s < live_slots, top, 0.0)
        col_out[pl.ds(c, 1), :] = jnp.maximum(col_out[pl.ds(c, 1), :], top)

    def gather(s, source):
        b = meta[0, jnp.maximum(s, 0)]
        best = jnp.max(source[...].T, axis=0, keepdims=True).astype(jnp.float32)
        best = jnp.where((s >= 0) & (s < live_slots), best, 0.0)
        row_out[pl.ds(b, 1), :] = jnp.maximum(row_out[pl.ds(b, 1), :], best)

    if weighted:
        for t in range(PER_COPY):
            turn(t, turned[0].at[t])

    def steps_from(target, base, wait):
        def step(k, carry):
            for odd in range(2):
                if wait:
                    fetch(2 * k + odd, target, base).wait()
            for odd in range(2):
                for t in range(PER_COPY):
                    s = (2 * k + odd) * PER_COPY + t
                    if weighted:
                        turn(jnp.minimum(s + PER_COPY, slots - 1), turned[1 - odd].at[t])
                    scale = turned[odd].at[t] if weighted else None
                    fold(s, target.at[s - base * PER_COPY], scale, folded[odd].at[t])
                    gather(s - PER_COPY, folded[1 - odd].at[t])
            return carry

        return step

    steps = (live_slots + 2 * PER_COPY - 1) // (2 * PER_COPY)
    half = own // 2
    lax.fori_loop(0, jnp.minimum(steps, half), steps_from(kept, 0, not weighted), 0)
    lax.fori_loop(half, steps, steps_from(held, own, True), 0)
    for t in range(PER_COPY):
        gather(steps * 2 * PER_COPY - PER_COPY + t, folded[1].at[t])

    def rest(target, base):
        def wait(k, carry):
            fetch(k, target, base).wait()
            return carry

        return wait

    if not weighted:
        lax.fori_loop(2 * jnp.minimum(steps, half), own, rest(kept, 0), 0)
    lax.fori_loop(2 * jnp.maximum(steps, half), fetched, rest(held, own), 0)


def sweep_call(tiles, meta, col_blocks, kept=None, scales=None):
    slots, width, _ = tiles.shape
    hbm = pl.BlockSpec(memory_space=pltpu.HBM)
    vmem = pl.BlockSpec(memory_space=pltpu.VMEM)
    weighted = kept is not None
    pair = (PER_COPY, width, LANES)
    folded = pltpu.VMEM(pair, jnp.float32 if weighted else FOLD1)
    turned = pltpu.VMEM(pair, jnp.float32)
    scratch = [
        pltpu.SMEM(meta.shape, meta.dtype),
        pltpu.VMEM((slots - KEPT, width, width), tiles.dtype),
        pltpu.SemaphoreType.DMA((slots // PER_COPY + 1,)),
        folded,
        folded,
    ]
    out_shape = [
        jax.ShapeDtypeStruct((BR_DEV, width), jnp.float32),
        jax.ShapeDtypeStruct((col_blocks, width), jnp.float32),
    ]
    if weighted:
        scratch += [pltpu.VMEM((width, LANES), jnp.bfloat16), turned, turned]
    else:
        out_shape.append(jax.ShapeDtypeStruct((KEPT, width, width), tiles.dtype))
    return pl.pallas_call(
        functools.partial(sweep_body, weighted),
        in_specs=[hbm] * 2 + [vmem] * (3 * weighted),
        out_specs=[vmem] * len(out_shape),
        out_shape=out_shape,
        scratch_shapes=scratch,
        compiler_params=pltpu.CompilerParams(vmem_limit_bytes=VMEM),
        name="weighted_sweep" if weighted else "first_sweep",
    )(meta, tiles, *((kept, *scales) if weighted else ()))


PROW = ("z", "core")
PCOL = ("y_pair", "y_side", "x")
Y = ("y_pair", "y_side")
NEAR = ((0, 7), (1, 2), (3, 4), (5, 6))
FAR = ((0, 3), (1, 6), (2, 5), (4, 7))


def from_everyone(value, axes):
    devices = lax.axis_size(axes)
    return lax.all_to_all(
        jnp.broadcast_to(value[None], (devices, *value.shape)), axes, 0, 0, tiled=True
    )


def with_partner(value, pairs):
    both = lax.all_gather(value, Y, axis=0, axis_index_groups=pairs)
    return jnp.maximum(both[0], both[1])


def rescale(scale, largest):
    return scale / jnp.sqrt(largest)


def on_device(tiles, tile_brow, tile_bcol, tile_count):
    slots = tiles.shape[2]
    width = tiles.shape[3]
    col_blocks = BR_DEV * lax.axis_size(PROW) // lax.axis_size(PCOL)
    block = tiles.reshape(slots, width, width)
    meta = jnp.concatenate(
        [
            tile_brow.reshape(1, slots),
            tile_bcol.reshape(1, slots),
            jnp.broadcast_to(tile_count, (1, 2 * slots)),
        ],
        axis=1,
    )
    row_vec = col_vec = None
    for sweep in range(SWEEPS):
        if sweep:
            row_max, col_max = sweep_call(block, meta, col_blocks, kept, (row_vec, col_vec))
        else:
            row_max, col_max, kept = sweep_call(block, meta, col_blocks)
        row_max = jnp.max(from_everyone(row_max, ("y_side", "x")), axis=0)
        row_max, col_max = lax.optimization_barrier((row_max, col_max))
        col_max = from_everyone(col_max, PROW)
        row_max = with_partner(row_max, NEAR)
        row_max = with_partner(row_max, FAR)
        row_max, col_max = lax.optimization_barrier((row_max, col_max))
        col_max = jnp.max(col_max, axis=0)
        if sweep:
            row_vec = rescale(row_vec, row_max)
            col_vec = rescale(col_vec, col_vec * col_max)
        else:
            row_vec = 1.0 / jnp.sqrt(row_max)
            col_vec = 1.0 / jnp.sqrt(col_max)
    return (row_vec.reshape(BR_DEV, 1, width), col_vec.reshape(col_blocks, 1, width))


def solution(mesh):
    shape = (mesh.shape["prow"] // 2, 2, mesh.shape["pcol"] // 8, 2, 4)
    finer = Mesh(mesh.devices.reshape(shape), PROW + PCOL)
    in_specs = (
        P(PROW, PCOL, None, None, None),
        P(PROW, PCOL, None),
        P(PROW, PCOL, None),
        P(PROW, PCOL),
    )
    out_specs = (P(None, PROW, None), P(None, PCOL, None))
    return jax.shard_map(
        on_device, mesh=finer, in_specs=in_specs, out_specs=out_specs, check_vma=False
    )
```

time: 117 us -> 110 us (0.940)
  blocking collectives: 74.7 us -> 70.1 us
  local copies, waits for them, and re-layouts: 4.82 us -> 3.51 us
  Pallas kernels: 6.92 us -> 5.62 us
    all_gather x6, blocking collectives: 42 us -> 36.5 us  [with_partner(): both = lax.all_gather(value, Y, axis=0, axis_index_groups=pairs)]
    unnamed x10 -> x2, local copies, waits for them, and re-layouts: 2.59 us -> 1.28 us
    pallas_call x3, Pallas kernels: 6.92 us -> 5.62 us  [sweep_call(): pl.pallas_call(functools.partial(sweep_body, weighted), in_specs=[hbm] *...]
where the time goes in v3:
time: 110 us; the launch traced here: 109 us
  blocking collectives  70.1 us (64%)
  starting transfers between devices  27.7 us (25%)
  Pallas kernels  5.62 us (5%)
  local copies, waits for them, and re-layouts  3.51 us (3%)
  between operations  1.45 us (1%)
    all_gather x6, blocking collectives, with_partner(): both = lax.all_gather(value, Y, axis=0, axis_index_groups=pairs)  36.5 us
    all_to_all x3, blocking collectives, from_everyone(): lax.all_to_all(jnp.broadcast_to(value[None], (devices, *value.shape)), ax...  33.6 us
    all_to_all x3, starting transfers between devices, from_everyone(): lax.all_to_all(jnp.broadcast_to(value[None], (devices, *value.shape)), ax...  27.7 us
    pallas_call x3, Pallas kernels, sweep_call(): pl.pallas_call(functools.partial(sweep_body, weighted), in_specs=[hbm] *...  5.62 us
    broadcast_in_dim x6, local copies, waits for them, and re-layouts, from_everyone(): jnp.broadcast_to(value[None], (devices, *value.shape))  2.21 us
  transfers between devices with their start and end apart: 3, of which 0 were waited for; matrix products, arithmetic and copies ran while one was open for 0% of the time, Pallas kernels for 0%

profile of v3, /device:TPU:16, one launch (start us, length us, event | category | flops | bytes accessed | tf_op | source)
XLA Modules:
  0.0 109.4 jit_solution(16732879849024913995)
XLA Ops:
  1.3 0.7 bitcast_add_fusion.meta_in
  2.0 2.3 %first_sweep.1 = (f32[32,256]{1,0:T(8,128)S(1)}, f32[16,256]{1,0:T(8,128)S(1)}, bf16[12,256,256]{2,1,0:T(8,128)(2,1)S(1)}) custom-call(s32[1,128]{1,0:T(1,128)S(1)} %bitcast_add_fusion.meta_in, bf16[32,256,256]{2,1,0:T(8,128)(2,1)} %bitcast.25), custom_call_target="tpu_custom_call" | custom-call | tf_op jit(solution)/shard_map/first_sweep/pallas_call | solution.py:169
  4.4 12.6 %all_to_all.30 = f32[8,32,256]{2,1,0:T(8,128)S(1)} all-to-all(f32[8,32,256]{2,1,0:T(8,128)S(1)} %broadcast_in_dim.18), channel_id=1, replica_groups=mesh['z'=8,'core'=2,'y_pair'=4,'y_side'=2,'x'=4] {'y_side','x'}, dimensions={0} | all-to-all | bytes 524288 | tf_op jit(solution)/shard_map/all_to_all | solution.py:189
  17.0 0.7 broadcast_in_dim.19
  17.7 11.5 %all-to-all-start.1 = ((f32[16,16,256]{2,1,0:T(8,128)}), f32[16,16,256]{2,1,0:T(8,128)S(1)}, u32[]{:S(2)}, u32[]{:S(2)}) async-start(f32[16,16,256]{2,1,0:T(8,128)} %broadcast_in_dim.19), calls=%async_computation.1 | async-start | bytes 524288 | tf_op jit(solution)/shard_map/all_to_all | solution.py:189
  29.2 4.6 %all-gather = f32[64,256]{1,0:T(8,128)S(1)} all-gather(f32[32,256]{1,0:T(8,128)S(1)} %reduce_max.58), channel_id=2, replica_groups={{0,28},{4,8},{12,16},{20,24},{1,29},{5,9},{13,17},{21,25},{2,30},{6,10}..., dimensions={0}, use_global_device_ids=true | all-gather | bytes 98304 | tf_op jit(solution)/shard_map/all_gather | solution.py:195
  33.8 7.6 %all-gather.3 = f32[64,256]{1,0:T(8,128)S(1)} all-gather(f32[32,256]{1,0:T(8,128)S(1)} %slice_maximum_fusion.5), channel_id=5, replica_groups={{0,12},{4,24},{8,20},{16,28},{1,13},{5,25},{9,21},{17,29},{2,14},{6,26}..., dimensions={0}, use_global_device_ids=true | all-gather | bytes 98304 | tf_op jit(solution)/shard_map/all_gather | solution.py:195
  41.4 0.0 all-to-all-done.1
  41.5 1.7 %weighted_sweep.2 = (f32[32,256]{1,0:T(8,128)S(1)}, f32[16,256]{1,0:T(8,128)S(1)}) custom-call(s32[1,128]{1,0:T(1,128)S(1)} %bitcast_add_fusion.meta_in, bf16[32,256,256]{2,1,0:T(8,128)(2,1)} %bitcast.26, bf16[12,256,256]{2,1,0:T(8,128)(2,1)S(1)} %get-tuple-element.26.refs_0_, f32[32,256]{1,0:T(8,128)S(1)} %sqrt.22.refs_1_, f32[16,256]{1,0:T(8,128)S(1)} %sqrt.23.refs_2_), custom_call_target="tpu_custom_call" | custom-call | tf_op jit(solution)/shard_map/weighted_sweep/pallas_call | solution.py:169
  43.2 10.5 %all_to_all.31 = f32[8,32,256]{2,1,0:T(8,128)S(1)} all-to-all(f32[8,32,256]{2,1,0:T(8,128)S(1)} %broadcast_in_dim.20), channel_id=1, replica_groups=mesh['z'=8,'core'=2,'y_pair'=4,'y_side'=2,'x'=4] {'y_side','x'}, dimensions={0} | all-to-all | bytes 524288 | tf_op jit(solution)/shard_map/all_to_all | solution.py:189
  53.7 0.7 broadcast_in_dim.21
  54.4 8.1 %all-to-all-start.3 = ((f32[16,16,256]{2,1,0:T(8,128)}), f32[16,16,256]{2,1,0:T(8,128)S(1)}, u32[]{:S(2)}, u32[]{:S(2)}) async-start(f32[16,16,256]{2,1,0:T(8,128)} %broadcast_in_dim.21), calls=%async_computation.3 | async-start | bytes 524288 | tf_op jit(solution)/shard_map/all_to_all | solution.py:189
  62.5 4.6 %all-gather.1 = f32[64,256]{1,0:T(8,128)S(1)} all-gather(f32[32,256]{1,0:T(8,128)S(1)} %reduce_max.60), channel_id=3, replica_groups={{0,28},{4,8},{12,16},{20,24},{1,29},{5,9},{13,17},{21,25},{2,30},{6,10}..., dimensions={0}, use_global_device_ids=true | all-gather | bytes 98304 | tf_op jit(solution)/shard_map/all_gather | solution.py:195
  67.1 7.6 %all-gather.4 = f32[64,256]{1,0:T(8,128)S(1)} all-gather(f32[32,256]{1,0:T(8,128)S(1)} %slice_maximum_fusion.3), channel_id=6, replica_groups={{0,12},{4,24},{8,20},{16,28},{1,13},{5,25},{9,21},{17,29},{2,14},{6,26}..., dimensions={0}, use_global_device_ids=true | all-gather | bytes 98304 | tf_op jit(solution)/shard_map/all_gather | solution.py:195
  74.7 0.0 all-to-all-done.3
  74.8 1.7 %weighted_sweep.3 = (f32[32,256]{1,0:T(8,128)S(1)}, f32[16,256]{1,0:T(8,128)S(1)}) custom-call(s32[1,128]{1,0:T(1,128)S(1)} %bitcast_add_fusion.meta_in, bf16[32,256,256]{2,1,0:T(8,128)(2,1)} %bitcast.27, bf16[12,256,256]{2,1,0:T(8,128)(2,1)S(1)} %get-tuple-element.26.refs_0_, f32[32,256]{1,0:T(8,128)S(1)} %rsqrt_multiply_fusion.refs_1_, ...), custom_call_target="tpu_custom_call" | custom-call | tf_op jit(solution)/shard_map/weighted_sweep/pallas_call | solution.py:169
  76.5 10.5 %all_to_all.32 = f32[8,32,256]{2,1,0:T(8,128)S(1)} all-to-all(f32[8,32,256]{2,1,0:T(8,128)S(1)} %broadcast_in_dim.22), channel_id=1, replica_groups=mesh['z'=8,'core'=2,'y_pair'=4,'y_side'=2,'x'=4] {'y_side','x'}, dimensions={0} | all-to-all | bytes 524288 | tf_op jit(solution)/shard_map/all_to_all | solution.py:189
  87.0 0.7 broadcast_in_dim.23
  87.7 8.1 %all-to-all-start.5 = ((f32[16,16,256]{2,1,0:T(8,128)}), f32[16,16,256]{2,1,0:T(8,128)S(1)}, u32[]{:S(2)}, u32[]{:S(2)}) async-start(f32[16,16,256]{2,1,0:T(8,128)} %broadcast_in_dim.23), calls=%async_computation.5 | async-start | bytes 524288 | tf_op jit(solution)/shard_map/all_to_all | solution.py:189
  95.8 4.6 %all-gather.2 = f32[64,256]{1,0:T(8,128)S(1)} all-gather(f32[32,256]{1,0:T(8,128)S(1)} %reduce_max.62), channel_id=4, replica_groups={{0,28},{4,8},{12,16},{20,24},{1,29},{5,9},{13,17},{21,25},{2,30},{6,10}..., dimensions={0}, use_global_device_ids=true | all-gather | bytes 98304 | tf_op jit(solution)/shard_map/all_gather | solution.py:195
  100.4 7.6 %all-gather.5 = f32[64,256]{1,0:T(8,128)S(1)} all-gather(f32[32,256]{1,0:T(8,128)S(1)} %slice_maximum_fusion.1), channel_id=7, replica_groups={{0,12},{4,24},{8,20},{16,28},{1,13},{5,25},{9,21},{17,29},{2,14},{6,26}..., dimensions={0}, use_global_device_ids=true | all-gather | bytes 98304 | tf_op jit(solution)/shard_map/all_gather | solution.py:195
  108.0 0.0 all-to-all-done.5
  108.0 0.6 copy.8
  108.7 0.6 copy.9
  (22 shorter events, 0.3 us)
Async XLA Ops:
  17.7 23.7 %all-to-all-start.1 = ((f32[16,16,256]{2,1,0:T(8,128)}), f32[16,16,256]{2,1,0:T(8,128)S(1)}, u32[]{:S(2)}, u32[]{:S(2)}) async-start(f32[16,16,256]{2,1,0:T(8,128)} %broadcast_in_dim.19), calls=%async_computation.1 | async-start | bytes 524288 | tf_op jit(solution)/shard_map/all_to_all | solution.py:189
  54.4 20.3 %all-to-all-start.3 = ((f32[16,16,256]{2,1,0:T(8,128)}), f32[16,16,256]{2,1,0:T(8,128)S(1)}, u32[]{:S(2)}, u32[]{:S(2)}) async-start(f32[16,16,256]{2,1,0:T(8,128)} %broadcast_in_dim.21), calls=%async_computation.3 | async-start | bytes 524288 | tf_op jit(solution)/shard_map/all_to_all | solution.py:189
  87.7 20.3 %all-to-all-start.5 = ((f32[16,16,256]{2,1,0:T(8,128)}), f32[16,16,256]{2,1,0:T(8,128)S(1)}, u32[]{:S(2)}, u32[]{:S(2)}) async-start(f32[16,16,256]{2,1,0:T(8,128)} %broadcast_in_dim.23), calls=%async_computation.5 | async-start | bytes 524288 | tf_op jit(solution)/shard_map/all_to_all | solution.py:189

commit v4 on v3

--- a/solution.py
+++ b/solution.py
@@ -13,7 +13,8 @@
 PER_COPY = 2
 ROWS = 64
 KEPT = 12
-FOLD1 = jnp.float32
+PACKED = 16
+FOLD1 = jnp.bfloat16
 LANES = 128
 VMEM = 52 * 2**20
 
@@ -43,21 +44,11 @@
     if not weighted:
         for k in range(own):
             fetch(k, kept, 0).start()
-        for k in range(own, copies):
-            fetch(k, held, own).start()
+    for k in range(own, copies):
+        fetch(k, held, own).start()
     row_out[...] = jnp.zeros(row_out.shape, jnp.float32)
     col_out[...] = jnp.zeros(col_out.shape, jnp.float32)
-    about.wait()
-    live_slots = meta[0, 2 * slots]
-    fetched = copies
-    if weighted:
-        fetched = jnp.where(live_slots > first, copies, own)
-
-        def get(k, carry):
-            fetch(k, held, own).start()
-            return carry
-
-        lax.fori_loop(own, fetched, get, 0)
+    if weighted:
         left = row_scale[...]
         parts = []
         for _ in range(3):
@@ -65,6 +56,8 @@
             left = left - parts[-1]
         parts.append(jnp.zeros((LANES - 3 * BR_DEV, width), jnp.float32))
         spread[...] = jnp.concatenate(parts, axis=0).T.astype(jnp.bfloat16)
+    about.wait()
+    live_slots = meta[0, 2 * slots]
 
     def turn(s, out):
         part = lax.broadcasted_iota(jnp.int32, (LANES, LANES), 0)
@@ -81,11 +74,12 @@
             best = None
             for side in range(2):
                 x = block[:, side * LANES : (side + 1) * LANES]
-                group = 16
                 if weighted:
                     x = x.astype(jnp.float32) * scale[pl.ds(h, ROWS), :]
-                    group = 8
-                down = jnp.max(x.reshape(ROWS // group, group, LANES), axis=0)
+                down = x
+                while down.shape[0] > PACKED:
+                    half = down.shape[0] // 2
+                    down = jnp.maximum(down[:half], down[half:])
                 tops[side] = down if tops[side] is None else jnp.maximum(tops[side], down)
                 if weighted:
                     x = x * weight[:, side * LANES : (side + 1) * LANES]
@@ -140,7 +134,7 @@
 
     if not weighted:
         lax.fori_loop(2 * jnp.minimum(steps, half), own, rest(kept, 0), 0)
-    lax.fori_loop(2 * jnp.maximum(steps, half), fetched, rest(held, own), 0)
+    lax.fori_loop(2 * jnp.maximum(steps, half), copies, rest(held, own), 0)
 
 
 def sweep_call(tiles, meta, col_blocks, kept=None, scales=None):
@@ -219,8 +213,9 @@
             row_max, col_max = sweep_call(block, meta, col_blocks, kept, (row_vec, col_vec))
         else:
             row_max, col_max, kept = sweep_call(block, meta, col_blocks)
-        row_max = jnp.max(from_everyone(row_max, ("y_side", "x")), axis=0)
+        row_max = from_everyone(row_max, ("y_side", "x"))
         row_max, col_max = lax.optimization_barrier((row_max, col_max))
+        row_max = jnp.max(row_max, axis=0)
         col_max = from_everyone(col_max, PROW)
         row_max = with_partner(row_max, NEAR)
         row_max = with_partner(row_max, FAR)

time: 110 us -> 109 us (level)
    all_to_all x3, blocking collectives: 33.6 us -> 32.3 us  [from_everyone(): lax.all_to_all(jnp.broadcast_to(value[None], (devices, *value.shape)), ax...]
where the time goes in v4:
time: 109 us; the launch traced here: 108 us
  blocking collectives  69.2 us (63%)
  starting transfers between devices  27.4 us (25%)
  Pallas kernels  5.91 us (5%)
  local copies, waits for them, and re-layouts  3.51 us (3%)
  between operations  1.46 us (1%)
    all_gather x6, blocking collectives, with_partner(): both = lax.all_gather(value, Y, axis=0, axis_index_groups=pairs)  36.8 us
    all_to_all x3, blocking collectives, from_everyone(): lax.all_to_all(jnp.broadcast_to(value[None], (devices, *value.shape)), ax...  32.3 us
    all_to_all x3, starting transfers between devices, from_everyone(): lax.all_to_all(jnp.broadcast_to(value[None], (devices, *value.shape)), ax...  27.4 us
    pallas_call x3, Pallas kernels, sweep_call(): pl.pallas_call(functools.partial(sweep_body, weighted), in_specs=[hbm] *...  5.91 us
    broadcast_in_dim x6, local copies, waits for them, and re-layouts, from_everyone(): jnp.broadcast_to(value[None], (devices, *value.shape))  2.21 us
  transfers between devices with their start and end apart: 3, of which 0 were waited for; matrix products, arithmetic and copies ran while one was open for 0% of the time, Pallas kernels for 0%

profile of v4, /device:TPU:16, one launch (start us, length us, event | category | flops | bytes accessed | tf_op | source)
XLA Modules:
  0.0 108.5 jit_solution(17602019472766773137)
XLA Ops:
  1.3 0.7 bitcast_add_fusion.meta_in
  2.0 2.3 %first_sweep.1 = (f32[32,256]{1,0:T(8,128)S(1)}, f32[16,256]{1,0:T(8,128)S(1)}, bf16[12,256,256]{2,1,0:T(8,128)(2,1)S(1)}) custom-call(s32[1,128]{1,0:T(1,128)S(1)} %bitcast_add_fusion.meta_in, bf16[32,256,256]{2,1,0:T(8,128)(2,1)} %bitcast.25), custom_call_target="tpu_custom_call" | custom-call | tf_op jit(solution)/shard_map/first_sweep/pallas_call | solution.py:163
  4.4 12.3 %all_to_all.30 = f32[8,32,256]{2,1,0:T(8,128)S(1)} all-to-all(f32[8,32,256]{2,1,0:T(8,128)S(1)} %broadcast_in_dim.18), channel_id=1, replica_groups=mesh['z'=8,'core'=2,'y_pair'=4,'y_side'=2,'x'=4] {'y_side','x'}, dimensions={0} | all-to-all | bytes 524288 | tf_op jit(solution)/shard_map/all_to_all | solution.py:183
  16.7 0.7 broadcast_in_dim.19
  17.4 11.1 %all-to-all-start.1 = ((f32[16,16,256]{2,1,0:T(8,128)}), f32[16,16,256]{2,1,0:T(8,128)S(1)}, u32[]{:S(2)}, u32[]{:S(2)}) async-start(f32[16,16,256]{2,1,0:T(8,128)} %broadcast_in_dim.19), calls=%async_computation.1 | async-start | bytes 524288 | tf_op jit(solution)/shard_map/all_to_all | solution.py:183
  28.6 4.6 %all-gather = f32[64,256]{1,0:T(8,128)S(1)} all-gather(f32[32,256]{1,0:T(8,128)S(1)} %reduce_max.58), channel_id=2, replica_groups={{0,28},{4,8},{12,16},{20,24},{1,29},{5,9},{13,17},{21,25},{2,30},{6,10}..., dimensions={0}, use_global_device_ids=true | all-gather | bytes 98304 | tf_op jit(solution)/shard_map/all_gather | solution.py:189
  33.2 7.9 %all-gather.3 = f32[64,256]{1,0:T(8,128)S(1)} all-gather(f32[32,256]{1,0:T(8,128)S(1)} %slice_maximum_fusion.5), channel_id=5, replica_groups={{0,12},{4,24},{8,20},{16,28},{1,13},{5,25},{9,21},{17,29},{2,14},{6,26}..., dimensions={0}, use_global_device_ids=true | all-gather | bytes 98304 | tf_op jit(solution)/shard_map/all_gather | solution.py:189
  41.1 0.0 all-to-all-done.1
  41.2 1.8 %weighted_sweep.2 = (f32[32,256]{1,0:T(8,128)S(1)}, f32[16,256]{1,0:T(8,128)S(1)}) custom-call(s32[1,128]{1,0:T(1,128)S(1)} %bitcast_add_fusion.meta_in, bf16[32,256,256]{2,1,0:T(8,128)(2,1)} %bitcast.26, bf16[12,256,256]{2,1,0:T(8,128)(2,1)S(1)} %get-tuple-element.26.refs_0_, f32[32,256]{1,0:T(8,128)S(1)} %sqrt.22.refs_1_, f32[16,256]{1,0:T(8,128)S(1)} %sqrt.23.refs_2_), custom_call_target="tpu_custom_call" | custom-call | tf_op jit(solution)/shard_map/weighted_sweep/pallas_call | solution.py:163
  43.0 9.8 %all_to_all.31 = f32[8,32,256]{2,1,0:T(8,128)S(1)} all-to-all(f32[8,32,256]{2,1,0:T(8,128)S(1)} %broadcast_in_dim.20), channel_id=1, replica_groups=mesh['z'=8,'core'=2,'y_pair'=4,'y_side'=2,'x'=4] {'y_side','x'}, dimensions={0} | all-to-all | bytes 524288 | tf_op jit(solution)/shard_map/all_to_all | solution.py:183
  52.9 0.7 broadcast_in_dim.21
  53.6 8.2 %all-to-all-start.3 = ((f32[16,16,256]{2,1,0:T(8,128)}), f32[16,16,256]{2,1,0:T(8,128)S(1)}, u32[]{:S(2)}, u32[]{:S(2)}) async-start(f32[16,16,256]{2,1,0:T(8,128)} %broadcast_in_dim.21), calls=%async_computation.3 | async-start | bytes 524288 | tf_op jit(solution)/shard_map/all_to_all | solution.py:183
  61.8 4.6 %all-gather.1 = f32[64,256]{1,0:T(8,128)S(1)} all-gather(f32[32,256]{1,0:T(8,128)S(1)} %reduce_max.60), channel_id=3, replica_groups={{0,28},{4,8},{12,16},{20,24},{1,29},{5,9},{13,17},{21,25},{2,30},{6,10}..., dimensions={0}, use_global_device_ids=true | all-gather | bytes 98304 | tf_op jit(solution)/shard_map/all_gather | solution.py:189
  66.4 7.6 %all-gather.4 = f32[64,256]{1,0:T(8,128)S(1)} all-gather(f32[32,256]{1,0:T(8,128)S(1)} %slice_maximum_fusion.3), channel_id=6, replica_groups={{0,12},{4,24},{8,20},{16,28},{1,13},{5,25},{9,21},{17,29},{2,14},{6,26}..., dimensions={0}, use_global_device_ids=true | all-gather | bytes 98304 | tf_op jit(solution)/shard_map/all_gather | solution.py:189
  74.0 0.0 all-to-all-done.3
  74.0 1.8 %weighted_sweep.3 = (f32[32,256]{1,0:T(8,128)S(1)}, f32[16,256]{1,0:T(8,128)S(1)}) custom-call(s32[1,128]{1,0:T(1,128)S(1)} %bitcast_add_fusion.meta_in, bf16[32,256,256]{2,1,0:T(8,128)(2,1)} %bitcast.27, bf16[12,256,256]{2,1,0:T(8,128)(2,1)S(1)} %get-tuple-element.26.refs_0_, f32[32,256]{1,0:T(8,128)S(1)} %rsqrt_multiply_fusion.refs_1_, ...), custom_call_target="tpu_custom_call" | custom-call | tf_op jit(solution)/shard_map/weighted_sweep/pallas_call | solution.py:163
  75.9 10.2 %all_to_all.32 = f32[8,32,256]{2,1,0:T(8,128)S(1)} all-to-all(f32[8,32,256]{2,1,0:T(8,128)S(1)} %broadcast_in_dim.22), channel_id=1, replica_groups=mesh['z'=8,'core'=2,'y_pair'=4,'y_side'=2,'x'=4] {'y_side','x'}, dimensions={0} | all-to-all | bytes 524288 | tf_op jit(solution)/shard_map/all_to_all | solution.py:183
  86.1 0.7 broadcast_in_dim.23
  86.8 8.1 %all-to-all-start.5 = ((f32[16,16,256]{2,1,0:T(8,128)}), f32[16,16,256]{2,1,0:T(8,128)S(1)}, u32[]{:S(2)}, u32[]{:S(2)}) async-start(f32[16,16,256]{2,1,0:T(8,128)} %broadcast_in_dim.23), calls=%async_computation.5 | async-start | bytes 524288 | tf_op jit(solution)/shard_map/all_to_all | solution.py:183
  94.9 4.6 %all-gather.2 = f32[64,256]{1,0:T(8,128)S(1)} all-gather(f32[32,256]{1,0:T(8,128)S(1)} %reduce_max.62), channel_id=4, replica_groups={{0,28},{4,8},{12,16},{20,24},{1,29},{5,9},{13,17},{21,25},{2,30},{6,10}..., dimensions={0}, use_global_device_ids=true | all-gather | bytes 98304 | tf_op jit(solution)/shard_map/all_gather | solution.py:189
  99.5 7.6 %all-gather.5 = f32[64,256]{1,0:T(8,128)S(1)} all-gather(f32[32,256]{1,0:T(8,128)S(1)} %slice_maximum_fusion.1), channel_id=7, replica_groups={{0,12},{4,24},{8,20},{16,28},{1,13},{5,25},{9,21},{17,29},{2,14},{6,26}..., dimensions={0}, use_global_device_ids=true | all-gather | bytes 98304 | tf_op jit(solution)/shard_map/all_gather | solution.py:189
  107.1 0.0 all-to-all-done.5
  107.1 0.6 copy.6
  107.8 0.6 copy.7
  (22 shorter events, 0.3 us)
Async XLA Ops:
  17.4 23.7 %all-to-all-start.1 = ((f32[16,16,256]{2,1,0:T(8,128)}), f32[16,16,256]{2,1,0:T(8,128)S(1)}, u32[]{:S(2)}, u32[]{:S(2)}) async-start(f32[16,16,256]{2,1,0:T(8,128)} %broadcast_in_dim.19), calls=%async_computation.1 | async-start | bytes 524288 | tf_op jit(solution)/shard_map/all_to_all | solution.py:183
  53.6 20.4 %all-to-all-start.3 = ((f32[16,16,256]{2,1,0:T(8,128)}), f32[16,16,256]{2,1,0:T(8,128)S(1)}, u32[]{:S(2)}, u32[]{:S(2)}) async-start(f32[16,16,256]{2,1,0:T(8,128)} %broadcast_in_dim.21), calls=%async_computation.3 | async-start | bytes 524288 | tf_op jit(solution)/shard_map/all_to_all | solution.py:183
  86.8 20.3 %all-to-all-start.5 = ((f32[16,16,256]{2,1,0:T(8,128)}), f32[16,16,256]{2,1,0:T(8,128)S(1)}, u32[]{:S(2)}, u32[]{:S(2)}) async-start(f32[16,16,256]{2,1,0:T(8,128)} %broadcast_in_dim.23), calls=%async_computation.5 | async-start | bytes 524288 | tf_op jit(solution)/shard_map/all_to_all | solution.py:183

commit v5 on v4

--- a/solution.py
+++ b/solution.py
@@ -21,10 +21,10 @@
 
 def sweep_body(weighted, meta_in, tiles, *refs):
     if weighted:
-        kept, row_scale, col_scale, row_out, col_out, *refs = refs
+        kept, row_scale, col_scale, row_out, col_all, *refs = refs
     else:
-        row_out, col_out, kept, *refs = refs
-    meta, held, sems, folded_a, folded_b, *refs = refs
+        row_out, col_all, kept, *refs = refs
+    meta, held, sems, col_sems, col_out, folded_a, folded_b, *refs = refs
     folded = (folded_a, folded_b)
     if weighted:
         spread, *turned = refs
@@ -122,8 +122,16 @@
     half = own // 2
     lax.fori_loop(0, jnp.minimum(steps, half), steps_from(kept, 0, not weighted), 0)
     lax.fori_loop(half, steps, steps_from(held, own, True), 0)
+    away = [
+        pltpu.make_async_copy(col_out, col_all.at[d], col_sems.at[d])
+        for d in range(col_all.shape[0])
+    ]
+    for copy in away:
+        copy.start()
     for t in range(PER_COPY):
         gather(steps * 2 * PER_COPY - PER_COPY + t, folded[1].at[t])
+    for copy in away:
+        copy.wait()
 
     def rest(target, base):
         def wait(k, carry):
@@ -137,7 +145,7 @@
     lax.fori_loop(2 * jnp.maximum(steps, half), copies, rest(held, own), 0)
 
 
-def sweep_call(tiles, meta, col_blocks, kept=None, scales=None):
+def sweep_call(tiles, meta, col_blocks, peers, kept=None, scales=None):
     slots, width, _ = tiles.shape
     hbm = pl.BlockSpec(memory_space=pltpu.HBM)
     vmem = pl.BlockSpec(memory_space=pltpu.VMEM)
@@ -149,12 +157,14 @@
         pltpu.SMEM(meta.shape, meta.dtype),
         pltpu.VMEM((slots - KEPT, width, width), tiles.dtype),
         pltpu.SemaphoreType.DMA((slots // PER_COPY + 1,)),
+        pltpu.SemaphoreType.DMA((peers,)),
+        pltpu.VMEM((col_blocks, width), jnp.float32),
         folded,
         folded,
     ]
     out_shape = [
         jax.ShapeDtypeStruct((BR_DEV, width), jnp.float32),
-        jax.ShapeDtypeStruct((col_blocks, width), jnp.float32),
+        jax.ShapeDtypeStruct((peers, col_blocks, width), jnp.float32),
     ]
     if weighted:
         scratch += [pltpu.VMEM((width, LANES), jnp.bfloat16), turned, turned]
@@ -163,7 +173,7 @@
     return pl.pallas_call(
         functools.partial(sweep_body, weighted),
         in_specs=[hbm] * 2 + [vmem] * (3 * weighted),
-        out_specs=[vmem] * len(out_shape),
+        out_specs=[vmem, hbm, vmem][: len(out_shape)],
         out_shape=out_shape,
         scratch_shapes=scratch,
         compiler_params=pltpu.CompilerParams(vmem_limit_bytes=VMEM),
@@ -207,16 +217,18 @@
         ],
         axis=1,
     )
+    peers = lax.axis_size(PROW)
     row_vec = col_vec = None
     for sweep in range(SWEEPS):
         if sweep:
-            row_max, col_max = sweep_call(block, meta, col_blocks, kept, (row_vec, col_vec))
+            scales = (row_vec, col_vec)
+            row_max, col_max = sweep_call(block, meta, col_blocks, peers, kept, scales)
         else:
-            row_max, col_max, kept = sweep_call(block, meta, col_blocks)
+            row_max, col_max, kept = sweep_call(block, meta, col_blocks, peers)
         row_max = from_everyone(row_max, ("y_side", "x"))
         row_max, col_max = lax.optimization_barrier((row_max, col_max))
         row_max = jnp.max(row_max, axis=0)
-        col_max = from_everyone(col_max, PROW)
+        col_max = lax.all_to_all(col_max, PROW, 0, 0, tiled=True)
         row_max = with_partner(row_max, NEAR)
         row_max = with_partner(row_max, FAR)
         row_max, col_max = lax.optimization_barrier((row_max, col_max))

time: 109 us -> 109 us (level)
  local copies, waits for them, and re-layouts: 3.51 us -> 1.35 us
  Pallas kernels: 5.91 us -> 7.05 us
    broadcast_in_dim x6 -> x3, local copies, waits for them, and re-layouts: 2.21 us -> 0.06 us  [from_everyone(): jnp.broadcast_to(value[None], (devices, *value.shape))]
    pallas_call x3, Pallas kernels: 5.91 us -> 7.05 us  [sweep_call(): pl.pallas_call(functools.partial(sweep_body, weighted), in_specs=[hbm] *...]
where the time goes in v5:
time: 109 us; the launch traced here: 108 us
  blocking collectives  70 us (64%)
  starting transfers between devices  27.6 us (25%)
  Pallas kernels  7.05 us (6%)
  between operations  1.46 us (1%)
  local copies, waits for them, and re-layouts  1.35 us (1%)
    all_gather x6, blocking collectives, with_partner(): both = lax.all_gather(value, Y, axis=0, axis_index_groups=pairs)  36.8 us
    all_to_all x3, blocking collectives, from_everyone(): lax.all_to_all(jnp.broadcast_to(value[None], (devices, *value.shape)), ax...  33.2 us
    all_to_all x3, starting transfers between devices, on_device(): col_max = lax.all_to_all(col_max, PROW, 0, 0, tiled=True)  27.6 us
    pallas_call x3, Pallas kernels, sweep_call(): pl.pallas_call(functools.partial(sweep_body, weighted), in_specs=[hbm] *...  7.05 us
  transfers between devices with their start and end apart: 3, of which 0 were waited for; matrix products, arithmetic and copies ran while one was open for 0% of the time, Pallas kernels for 0%

profile of v5, /device:TPU:16, one launch (start us, length us, event | category | flops | bytes accessed | tf_op | source)
XLA Modules:
  0.0 108.3 jit_solution(8063464077854649254)
XLA Ops:
  1.3 0.7 bitcast_add_fusion.meta_in
  2.0 2.5 %first_sweep.1 = (f32[32,256]{1,0:T(8,128)S(1)}, f32[16,16,256]{2,1,0:T(8,128)}, bf16[12,256,256]{2,1,0:T(8,128)(2,1)S(1)}) custom-call(s32[1,128]{1,0:T(1,128)S(1)} %bitcast_add_fusion.meta_in, bf16[32,256,256]{2,1,0:T(8,128)(2,1)} %bitcast.25), custom_call_target="tpu_custom_call" | custom-call | tf_op jit(solution)/shard_map/first_sweep/pallas_call | solution.py:173
  4.5 12.7 %all_to_all.30 = f32[8,32,256]{2,1,0:T(8,128)S(1)} all-to-all(f32[8,32,256]{2,1,0:T(8,128)S(1)} %broadcast_in_dim.12), channel_id=1, replica_groups=mesh['z'=8,'core'=2,'y_pair'=4,'y_side'=2,'x'=4] {'y_side','x'}, dimensions={0} | all-to-all | bytes 524288 | tf_op jit(solution)/shard_map/all_to_all | solution.py:193
  17.3 11.3 %all-to-all-start.1 = ((f32[16,16,256]{2,1,0:T(8,128)}), f32[16,16,256]{2,1,0:T(8,128)S(1)}, u32[]{:S(2)}, u32[]{:S(2)}) async-start(f32[16,16,256]{2,1,0:T(8,128)} %get-tuple-element.24), calls=%async_computation.1 | async-start | bytes 524288 | tf_op jit(solution)/shard_map/all_to_all | solution.py:231
  28.6 4.6 %all-gather = f32[64,256]{1,0:T(8,128)S(1)} all-gather(f32[32,256]{1,0:T(8,128)S(1)} %reduce_max.58), channel_id=2, replica_groups={{0,28},{4,8},{12,16},{20,24},{1,29},{5,9},{13,17},{21,25},{2,30},{6,10}..., dimensions={0}, use_global_device_ids=true | all-gather | bytes 98304 | tf_op jit(solution)/shard_map/all_gather | solution.py:199
  33.2 7.8 %all-gather.3 = f32[64,256]{1,0:T(8,128)S(1)} all-gather(f32[32,256]{1,0:T(8,128)S(1)} %slice_maximum_fusion.5), channel_id=5, replica_groups={{0,12},{4,24},{8,20},{16,28},{1,13},{5,25},{9,21},{17,29},{2,14},{6,26}..., dimensions={0}, use_global_device_ids=true | all-gather | bytes 98304 | tf_op jit(solution)/shard_map/all_gather | solution.py:199
  41.0 0.0 all-to-all-done.1
  41.1 2.3 %weighted_sweep.2 = (f32[32,256]{1,0:T(8,128)S(1)}, f32[16,16,256]{2,1,0:T(8,128)}) custom-call(s32[1,128]{1,0:T(1,128)S(1)} %bitcast_add_fusion.meta_in, bf16[32,256,256]{2,1,0:T(8,128)(2,1)} %bitcast.26, bf16[12,256,256]{2,1,0:T(8,128)(2,1)S(1)} %get-tuple-element.26.refs_0_, f32[32,256]{1,0:T(8,128)S(1)} %sqrt.22.refs_1_, f32[16,256]{1,0:T(8,128)S(1)} %sqrt.23.refs_2_), custom_call_target="tpu_custom_call" | custom-call | tf_op jit(solution)/shard_map/weighted_sweep/pallas_call | solution.py:173
  43.4 10.1 %all_to_all.31 = f32[8,32,256]{2,1,0:T(8,128)S(1)} all-to-all(f32[8,32,256]{2,1,0:T(8,128)S(1)} %broadcast_in_dim.13), channel_id=1, replica_groups=mesh['z'=8,'core'=2,'y_pair'=4,'y_side'=2,'x'=4] {'y_side','x'}, dimensions={0} | all-to-all | bytes 524288 | tf_op jit(solution)/shard_map/all_to_all | solution.py:193
  53.5 8.1 %all-to-all-start.3 = ((f32[16,16,256]{2,1,0:T(8,128)}), f32[16,16,256]{2,1,0:T(8,128)S(1)}, u32[]{:S(2)}, u32[]{:S(2)}) async-start(f32[16,16,256]{2,1,0:T(8,128)} %get-tuple-element.31), calls=%async_computation.3 | async-start | bytes 524288 | tf_op jit(solution)/shard_map/all_to_all | solution.py:231
  61.7 4.6 %all-gather.1 = f32[64,256]{1,0:T(8,128)S(1)} all-gather(f32[32,256]{1,0:T(8,128)S(1)} %reduce_max.60), channel_id=3, replica_groups={{0,28},{4,8},{12,16},{20,24},{1,29},{5,9},{13,17},{21,25},{2,30},{6,10}..., dimensions={0}, use_global_device_ids=true | all-gather | bytes 98304 | tf_op jit(solution)/shard_map/all_gather | solution.py:199
  66.3 7.6 %all-gather.4 = f32[64,256]{1,0:T(8,128)S(1)} all-gather(f32[32,256]{1,0:T(8,128)S(1)} %slice_maximum_fusion.3), channel_id=6, replica_groups={{0,12},{4,24},{8,20},{16,28},{1,13},{5,25},{9,21},{17,29},{2,14},{6,26}..., dimensions={0}, use_global_device_ids=true | all-gather | bytes 98304 | tf_op jit(solution)/shard_map/all_gather | solution.py:199
  73.9 0.0 all-to-all-done.3
  73.9 2.3 %weighted_sweep.3 = (f32[32,256]{1,0:T(8,128)S(1)}, f32[16,16,256]{2,1,0:T(8,128)}) custom-call(s32[1,128]{1,0:T(1,128)S(1)} %bitcast_add_fusion.meta_in, bf16[32,256,256]{2,1,0:T(8,128)(2,1)} %bitcast.27, bf16[12,256,256]{2,1,0:T(8,128)(2,1)S(1)} %get-tuple-element.26.refs_0_, f32[32,256]{1,0:T(8,128)S(1)} %rsqrt_multiply_fusion.refs_1_, ...), custom_call_target="tpu_custom_call" | custom-call | tf_op jit(solution)/shard_map/weighted_sweep/pallas_call | solution.py:173
  76.3 10.4 %all_to_all.32 = f32[8,32,256]{2,1,0:T(8,128)S(1)} all-to-all(f32[8,32,256]{2,1,0:T(8,128)S(1)} %broadcast_in_dim.14), channel_id=1, replica_groups=mesh['z'=8,'core'=2,'y_pair'=4,'y_side'=2,'x'=4] {'y_side','x'}, dimensions={0} | all-to-all | bytes 524288 | tf_op jit(solution)/shard_map/all_to_all | solution.py:193
  86.6 8.2 %all-to-all-start.5 = ((f32[16,16,256]{2,1,0:T(8,128)}), f32[16,16,256]{2,1,0:T(8,128)S(1)}, u32[]{:S(2)}, u32[]{:S(2)}) async-start(f32[16,16,256]{2,1,0:T(8,128)} %get-tuple-element.37), calls=%async_computation.5 | async-start | bytes 524288 | tf_op jit(solution)/shard_map/all_to_all | solution.py:231
  94.8 4.6 %all-gather.2 = f32[64,256]{1,0:T(8,128)S(1)} all-gather(f32[32,256]{1,0:T(8,128)S(1)} %reduce_max.62), channel_id=4, replica_groups={{0,28},{4,8},{12,16},{20,24},{1,29},{5,9},{13,17},{21,25},{2,30},{6,10}..., dimensions={0}, use_global_device_ids=true | all-gather | bytes 98304 | tf_op jit(solution)/shard_map/all_gather | solution.py:199
  99.4 7.6 %all-gather.5 = f32[64,256]{1,0:T(8,128)S(1)} all-gather(f32[32,256]{1,0:T(8,128)S(1)} %slice_maximum_fusion.1), channel_id=7, replica_groups={{0,12},{4,24},{8,20},{16,28},{1,13},{5,25},{9,21},{17,29},{2,14},{6,26}..., dimensions={0}, use_global_device_ids=true | all-gather | bytes 98304 | tf_op jit(solution)/shard_map/all_gather | solution.py:199
  107.0 0.0 all-to-all-done.5
  107.0 0.6 copy.6
  107.7 0.6 copy.7
  (22 shorter events, 0.3 us)
Async XLA Ops:
  17.3 23.7 %all-to-all-start.1 = ((f32[16,16,256]{2,1,0:T(8,128)}), f32[16,16,256]{2,1,0:T(8,128)S(1)}, u32[]{:S(2)}, u32[]{:S(2)}) async-start(f32[16,16,256]{2,1,0:T(8,128)} %get-tuple-element.24), calls=%async_computation.1 | async-start | bytes 524288 | tf_op jit(solution)/shard_map/all_to_all | solution.py:231
  53.5 20.4 %all-to-all-start.3 = ((f32[16,16,256]{2,1,0:T(8,128)}), f32[16,16,256]{2,1,0:T(8,128)S(1)}, u32[]{:S(2)}, u32[]{:S(2)}) async-start(f32[16,16,256]{2,1,0:T(8,128)} %get-tuple-element.31), calls=%async_computation.3 | async-start | bytes 524288 | tf_op jit(solution)/shard_map/all_to_all | solution.py:231
  86.6 20.4 %all-to-all-start.5 = ((f32[16,16,256]{2,1,0:T(8,128)}), f32[16,16,256]{2,1,0:T(8,128)S(1)}, u32[]{:S(2)}, u32[]{:S(2)}) async-start(f32[16,16,256]{2,1,0:T(8,128)} %get-tuple-element.37), calls=%async_computation.5 | async-start | bytes 524288 | tf_op jit(solution)/shard_map/all_to_all | solution.py:231

commit v6 on v5

--- a/solution.py
+++ b/solution.py
@@ -181,6 +181,26 @@
     )(meta, tiles, *((kept, *scales) if weighted else ()))
 
 
+def last_body(row_scale, col_scale, row_max, col_all, row_out, col_out):
+    col_max = jnp.max(col_all[...], axis=0)
+    row_out[:, 0, :] = rescale(row_scale[...], row_max[...])
+    col_out[:, 0, :] = rescale(col_scale[...], col_scale[...] * col_max)
+
+
+def last_call(*operands):
+    vmem = pl.BlockSpec(memory_space=pltpu.VMEM)
+    return pl.pallas_call(
+        last_body,
+        in_specs=[vmem] * 4,
+        out_specs=[vmem] * 2,
+        out_shape=[
+            jax.ShapeDtypeStruct((x.shape[0], 1, x.shape[1]), jnp.float32) for x in operands[:2]
+        ],
+        compiler_params=pltpu.CompilerParams(vmem_limit_bytes=VMEM),
+        name="last_scales",
+    )(*operands)
+
+
 PROW = ("z", "core")
 PCOL = ("y_pair", "y_side", "x")
 Y = ("y_pair", "y_side")
@@ -225,13 +245,15 @@
             row_max, col_max = sweep_call(block, meta, col_blocks, peers, kept, scales)
         else:
             row_max, col_max, kept = sweep_call(block, meta, col_blocks, peers)
-        row_max = from_everyone(row_max, ("y_side", "x"))
+        row_max = from_everyone(row_max, ("x", "y_side"))
         row_max, col_max = lax.optimization_barrier((row_max, col_max))
         row_max = jnp.max(row_max, axis=0)
-        col_max = lax.all_to_all(col_max, PROW, 0, 0, tiled=True)
+        col_max = lax.all_to_all(col_max, ("core", "z"), 0, 0, tiled=True)
         row_max = with_partner(row_max, NEAR)
         row_max = with_partner(row_max, FAR)
         row_max, col_max = lax.optimization_barrier((row_max, col_max))
+        if sweep == SWEEPS - 1:
+            return tuple(last_call(row_vec, col_vec, row_max, col_max))
         col_max = jnp.max(col_max, axis=0)
         if sweep:
             row_vec = rescale(row_vec, row_max)
@@ -239,7 +261,6 @@
         else:
             row_vec = 1.0 / jnp.sqrt(row_max)
             col_vec = 1.0 / jnp.sqrt(col_max)
-    return (row_vec.reshape(BR_DEV, 1, width), col_vec.reshape(col_blocks, 1, width))
 
 
 def solution(mesh):

time: 109 us -> 109 us (level)
  local copies, waits for them, and re-layouts: 1.35 us -> 0.08 us
    unnamed x2 -> x0, local copies, waits for them, and re-layouts: 1.28 us -> none
where the time goes in v6:
time: 109 us; the launch traced here: 108 us
  blocking collectives  69.9 us (64%)
  starting transfers between devices  28.1 us (26%)
  Pallas kernels  7.71 us (7%)
  between operations  1.44 us (1%)
    all_gather x6, blocking collectives, with_partner(): both = lax.all_gather(value, Y, axis=0, axis_index_groups=pairs)  36.9 us
    all_to_all x3, blocking collectives, from_everyone(): lax.all_to_all(jnp.broadcast_to(value[None], (devices, *value.shape)), ax...  33 us
    all_to_all x3, starting transfers between devices, on_device(): col_max = lax.all_to_all(col_max, ('core', 'z'), 0, 0, tiled=True)  28.1 us
    pallas_call x3, Pallas kernels, sweep_call(): pl.pallas_call(functools.partial(sweep_body, weighted), in_specs=[hbm] *...  7.05 us
  transfers between devices with their start and end apart: 3, of which 0 were waited for; matrix products, arithmetic and copies ran while one was open for 0% of the time, Pallas kernels for 0%

profile of v6, /device:TPU:16, one launch (start us, length us, event | category | flops | bytes accessed | tf_op | source)
XLA Modules:
  0.0 108.1 jit_solution(11095353478368573616)
XLA Ops:
  1.3 0.7 bitcast_add_fusion.meta_in
  2.0 2.5 %first_sweep.1 = (f32[32,256]{1,0:T(8,128)S(1)}, f32[16,16,256]{2,1,0:T(8,128)}, bf16[12,256,256]{2,1,0:T(8,128)(2,1)S(1)}) custom-call(s32[1,128]{1,0:T(1,128)S(1)} %bitcast_add_fusion.meta_in, bf16[32,256,256]{2,1,0:T(8,128)(2,1)} %bitcast.7), custom_call_target="tpu_custom_call" | custom-call | tf_op jit(solution)/shard_map/first_sweep/pallas_call | solution.py:173
  4.5 12.8 %all_to_all.30 = f32[8,32,256]{2,1,0:T(8,128)S(1)} all-to-all(f32[8,32,256]{2,1,0:T(8,128)S(1)} %broadcast_in_dim.12), channel_id=1, replica_groups=mesh['z'=8,'core'=2,'y_pair'=4,'y_side'=2,'x'=4] {'x','y_side'}, dimensions={0} | all-to-all | bytes 524288 | tf_op jit(solution)/shard_map/all_to_all | solution.py:213
  17.3 11.3 %all-to-all-start.1 = ((f32[16,16,256]{2,1,0:T(8,128)}), f32[16,16,256]{2,1,0:T(8,128)S(1)}, u32[]{:S(2)}, u32[]{:S(2)}) async-start(f32[16,16,256]{2,1,0:T(8,128)} %get-tuple-element.24), calls=%async_computation.1 | async-start | bytes 524288 | tf_op jit(solution)/shard_map/all_to_all | solution.py:251
  28.6 4.6 %all-gather = f32[64,256]{1,0:T(8,128)S(1)} all-gather(f32[32,256]{1,0:T(8,128)S(1)} %reduce_max.45), channel_id=2, replica_groups={{0,28},{4,8},{12,16},{20,24},{1,29},{5,9},{13,17},{21,25},{2,30},{6,10}..., dimensions={0}, use_global_device_ids=true | all-gather | bytes 98304 | tf_op jit(solution)/shard_map/all_gather | solution.py:219
  33.2 7.8 %all-gather.3 = f32[64,256]{1,0:T(8,128)S(1)} all-gather(f32[32,256]{1,0:T(8,128)S(1)} %slice_maximum_fusion.5), channel_id=5, replica_groups={{0,12},{4,24},{8,20},{16,28},{1,13},{5,25},{9,21},{17,29},{2,14},{6,26}..., dimensions={0}, use_global_device_ids=true | all-gather | bytes 98304 | tf_op jit(solution)/shard_map/all_gather | solution.py:219
  41.1 0.0 all-to-all-done.1
  41.1 2.3 %weighted_sweep.2 = (f32[32,256]{1,0:T(8,128)S(1)}, f32[16,16,256]{2,1,0:T(8,128)}) custom-call(s32[1,128]{1,0:T(1,128)S(1)} %bitcast_add_fusion.meta_in, bf16[32,256,256]{2,1,0:T(8,128)(2,1)} %bitcast.8, bf16[12,256,256]{2,1,0:T(8,128)(2,1)S(1)} %get-tuple-element.26.refs_0_, f32[32,256]{1,0:T(8,128)S(1)} %sqrt.12.refs_1_, f32[16,256]{1,0:T(8,128)S(1)} %sqrt.13.refs_2_), custom_call_target="tpu_custom_call" | custom-call | tf_op jit(solution)/shard_map/weighted_sweep/pallas_call | solution.py:173
  43.5 10.0 %all_to_all.31 = f32[8,32,256]{2,1,0:T(8,128)S(1)} all-to-all(f32[8,32,256]{2,1,0:T(8,128)S(1)} %broadcast_in_dim.13), channel_id=1, replica_groups=mesh['z'=8,'core'=2,'y_pair'=4,'y_side'=2,'x'=4] {'x','y_side'}, dimensions={0} | all-to-all | bytes 524288 | tf_op jit(solution)/shard_map/all_to_all | solution.py:213
  53.4 8.5 %all-to-all-start.3 = ((f32[16,16,256]{2,1,0:T(8,128)}), f32[16,16,256]{2,1,0:T(8,128)S(1)}, u32[]{:S(2)}, u32[]{:S(2)}) async-start(f32[16,16,256]{2,1,0:T(8,128)} %get-tuple-element.31), calls=%async_computation.3 | async-start | bytes 524288 | tf_op jit(solution)/shard_map/all_to_all | solution.py:251
  61.9 4.6 %all-gather.1 = f32[64,256]{1,0:T(8,128)S(1)} all-gather(f32[32,256]{1,0:T(8,128)S(1)} %reduce_max.47), channel_id=3, replica_groups={{0,28},{4,8},{12,16},{20,24},{1,29},{5,9},{13,17},{21,25},{2,30},{6,10}..., dimensions={0}, use_global_device_ids=true | all-gather | bytes 98304 | tf_op jit(solution)/shard_map/all_gather | solution.py:219
  66.5 7.6 %all-gather.4 = f32[64,256]{1,0:T(8,128)S(1)} all-gather(f32[32,256]{1,0:T(8,128)S(1)} %slice_maximum_fusion.3), channel_id=6, replica_groups={{0,12},{4,24},{8,20},{16,28},{1,13},{5,25},{9,21},{17,29},{2,14},{6,26}..., dimensions={0}, use_global_device_ids=true | all-gather | bytes 98304 | tf_op jit(solution)/shard_map/all_gather | solution.py:219
  74.1 0.0 all-to-all-done.3
  74.2 2.3 %weighted_sweep.3 = (f32[32,256]{1,0:T(8,128)S(1)}, f32[16,16,256]{2,1,0:T(8,128)}) custom-call(s32[1,128]{1,0:T(1,128)S(1)} %bitcast_add_fusion.meta_in, bf16[32,256,256]{2,1,0:T(8,128)(2,1)} %bitcast.9, bf16[12,256,256]{2,1,0:T(8,128)(2,1)S(1)} %get-tuple-element.26.refs_0_, f32[32,256]{1,0:T(8,128)S(1)} %rsqrt_multiply_fusion.refs_1_.row_scale, ...), custom_call_target="tpu_custom_call" | custom-call | tf_op jit(solution)/shard_map/weighted_sweep/pallas_call | solution.py:173
  76.5 10.2 %all_to_all.32 = f32[8,32,256]{2,1,0:T(8,128)S(1)} all-to-all(f32[8,32,256]{2,1,0:T(8,128)S(1)} %broadcast_in_dim.14), channel_id=1, replica_groups=mesh['z'=8,'core'=2,'y_pair'=4,'y_side'=2,'x'=4] {'x','y_side'}, dimensions={0} | all-to-all | bytes 524288 | tf_op jit(solution)/shard_map/all_to_all | solution.py:213
  86.7 8.3 %all-to-all-start.5 = ((f32[16,16,256]{2,1,0:T(8,128)}), f32[16,16,256]{2,1,0:T(8,128)S(1)}, u32[]{:S(2)}, u32[]{:S(2)}) async-start(f32[16,16,256]{2,1,0:T(8,128)} %get-tuple-element.37), calls=%async_computation.5 | async-start | bytes 524288 | tf_op jit(solution)/shard_map/all_to_all | solution.py:251
  95.1 4.6 %all-gather.2 = f32[64,256]{1,0:T(8,128)S(1)} all-gather(f32[32,256]{1,0:T(8,128)S(1)} %reduce_max.49), channel_id=4, replica_groups={{0,28},{4,8},{12,16},{20,24},{1,29},{5,9},{13,17},{21,25},{2,30},{6,10}..., dimensions={0}, use_global_device_ids=true | all-gather | bytes 98304 | tf_op jit(solution)/shard_map/all_gather | solution.py:219
  99.7 7.7 %all-gather.5 = f32[64,256]{1,0:T(8,128)S(1)} all-gather(f32[32,256]{1,0:T(8,128)S(1)} %slice_maximum_fusion.1), channel_id=7, replica_groups={{0,12},{4,24},{8,20},{16,28},{1,13},{5,25},{9,21},{17,29},{2,14},{6,26}..., dimensions={0}, use_global_device_ids=true | all-gather | bytes 98304 | tf_op jit(solution)/shard_map/all_gather | solution.py:219
  107.4 0.0 all-to-all-done.5.col_all
  107.4 0.7 last_scales.1
  (19 shorter events, 0.2 us)
Async XLA Ops:
  17.3 23.7 %all-to-all-start.1 = ((f32[16,16,256]{2,1,0:T(8,128)}), f32[16,16,256]{2,1,0:T(8,128)S(1)}, u32[]{:S(2)}, u32[]{:S(2)}) async-start(f32[16,16,256]{2,1,0:T(8,128)} %get-tuple-element.24), calls=%async_computation.1 | async-start | bytes 524288 | tf_op jit(solution)/shard_map/all_to_all | solution.py:251
  53.4 20.7 %all-to-all-start.3 = ((f32[16,16,256]{2,1,0:T(8,128)}), f32[16,16,256]{2,1,0:T(8,128)S(1)}, u32[]{:S(2)}, u32[]{:S(2)}) async-start(f32[16,16,256]{2,1,0:T(8,128)} %get-tuple-element.31), calls=%async_computation.3 | async-start | bytes 524288 | tf_op jit(solution)/shard_map/all_to_all | solution.py:251
  86.7 20.7 %all-to-all-start.5 = ((f32[16,16,256]{2,1,0:T(8,128)}), f32[16,16,256]{2,1,0:T(8,128)S(1)}, u32[]{:S(2)}, u32[]{:S(2)}) async-start(f32[16,16,256]{2,1,0:T(8,128)} %get-tuple-element.37), calls=%async_computation.5 | async-start | bytes 524288 | tf_op jit(solution)/shard_map/all_to_all | solution.py:251
